TPU v7x, 256 devices: a whole 4x4x8 slice. The times are simulated.
256 devices in a mesh: vox: 64 (over x, y, z_hi), fil: 4 (over z_lo, core).
Axes of the slice: x: 4, y: 4, z: 8 (z_hi: 4, z_lo: 2; z = z_hi * 2 + z_lo), core: 2. Of those that a mesh axis runs over, the one named last changes fastest.
Arguments:
- volume: bfloat16 [16, 128, 128, 256], P(None, 'vox', 'fil'), may hold values from -6 to 6
- fine_kernel: bfloat16 [16, 16, 3, 3, 3], replicated, may hold values from -0.3125 to 0.3125
- coarse_kernel: bfloat16 [64, 16, 3, 3, 3], replicated, may hold values from -0.3125 to 0.3125
- coarse_cot: bfloat16 [64, 64, 64, 128], P('fil', 'vox'), may hold values from -0.03125 to 0.03125
Outputs:
- coarse_out: bfloat16 [64, 64, 64, 128], P('fil', 'vox')
- grad_fine: float32 [16, 16, 3, 3, 3], replicated
- grad_coarse: float32 [64, 16, 3, 3, 3], replicated
All inputs are finite; a program needn't handle non-finite values.
Results may differ from a plain program's by a relative error of at most 0.006.
Values may be sent and summed in bfloat16 or wider, within the bound.
No kernel may reach another device: no remote copies, remote signals or barrier semaphores. Data moves between devices by JAX's collectives and lax.ppermute only.
A program may use at most 128 MiB of HBM per device.

v0:
```python
import functools

import jax
import jax.numpy as jnp
from jax import lax
from jax.experimental import pallas as pl
from jax.experimental.pallas import tpu as pltpu
from jax.sharding import PartitionSpec as P


F32 = jnp.float32
BF16 = jnp.bfloat16
VMEM = pl.BlockSpec(memory_space=pltpu.VMEM)
HBM = pl.BlockSpec(memory_space=pltpu.HBM)


def dot(a, b):
    return lax.dot_general(a, b, (((1,), (0,)), ((), ())), preferred_element_type=F32)


def dot_t(a, b):
    return lax.dot_general(a, b, (((1,), (1,)), ((), ())), preferred_element_type=F32)


def iota(shape, dim):
    return lax.broadcasted_iota(jnp.int32, shape, dim)


def position():
    return lax.axis_index("fil"), lax.rem(lax.axis_index("vox"), 2)


def swap_matrix():
    row, col = iota((256, 256), 0), iota((256, 256), 1)
    return jnp.where(col == (row % 16) * 16 + row // 16, 1.0, 0.0).astype(BF16)


def roll_left(x, amount):
    return x if amount == 0 else pltpu.roll(x, x.shape[1] - amount, 1)


def moved(x, step):
    if step == 0:
        return x
    width = x.shape[1]
    edge = 0 if step == 1 else width - 1
    return jnp.where(iota(x.shape, 1) == edge, 0.0, pltpu.roll(x, step % width, 1))


def call(body, outs, scratch=(), flops=2_000_000_000, n_in=1, spec=VMEM, name=None):
    specs = [spec] * n_in
    return pl.pallas_call(
        body,
        out_shape=tuple(jax.ShapeDtypeStruct(s, d) for s, d in outs),
        in_specs=specs,
        out_specs=tuple(VMEM for _ in outs),
        scratch_shapes=scratch,
        cost_estimate=pl.CostEstimate(flops=flops, bytes_accessed=1_000_000, transcendentals=0),
        compiler_params=pltpu.CompilerParams(vmem_limit_bytes=32 * 1024 * 1024),
        name=name,
    )


def pack_kernel(vol_hbm, cot_hbm, near_ref, far_ref, pay_ref, vol_ref, cot_ref, sems):
    fil, odd = position()
    loads = [
        pltpu.make_async_copy(vol_hbm, vol_ref, sems.at[0]),
        pltpu.make_async_copy(cot_hbm, cot_ref, sems.at[1]),
    ]
    for load in loads:
        load.start()
    swap = swap_matrix()
    planes = (near_ref, far_ref)
    loads[0].wait()
    for which, v_ref in enumerate(planes):
        x = 1 - odd if which == 0 else odd
        for half in range(2):
            block = vol_ref[:, pl.ds(x, 1), 16 * half : 16 * half + 16, :].reshape(256, 256)
            v_ref[16 * half : 16 * half + 16] = dot(swap, block).astype(BF16).reshape(16, 16, 256)
    loads[1].wait()
    for dest in range(4):
        block = cot_ref[:, 0, 16 * dest : 16 * dest + 16, :].reshape(256, 128)
        rows = dot(swap, block).astype(BF16).reshape(16, 16, 128)
        pay_ref[dest, 1:17] = rows
        if dest < 3:
            pay_ref[dest + 1, 0] = rows[15]
        else:
            pay_ref[0, 0] = jnp.zeros((16, 128), BF16)
        if dest > 0:
            pay_ref[dest - 1, 17] = rows[0]
        else:
            pay_ref[3, 17] = jnp.zeros((16, 128), BF16)
    for dest in range(4):
        for which, v_ref in enumerate(planes):
            for side in range(2):
                at = 18 + 6 * side + 3 * which
                lanes = slice(128 * side, 128 * side + 128)
                rows = jnp.where(dest > fil, v_ref[29:32, :, lanes], v_ref[0:3, :, lanes])
                pay_ref[dest, at : at + 3] = rows


def weights_kernel(fk_ref, ck_ref, w1_ref, w2_ref, w4_ref):
    row, col = iota((64, 256), 0), iota((64, 256), 1)
    for slot in range(2):
        total = None
        for dy in range(3):
            place = jnp.where(col == (row // 16) * 64 + (slot + 2 - dy) * 16 + row % 16, 1.0, 0.0).astype(BF16)
            part = dot(ck_ref[:, dy].reshape(144, 64), place)
            total = part if total is None else total + part
        w1_ref[144 * slot : 144 * slot + 144] = total.astype(BF16)
    row, col = iota((16, 256), 0), iota((16, 256), 1)
    total = None
    for dx in range(3):
        for dy in range(3):
            place = jnp.where(col == row + 64 * dx + 16 * dy, 1.0, 0.0).astype(BF16)
            part = dot(fk_ref[dx, dy].reshape(48, 16), place)
            total = part if total is None else total + part
    for x in range(2):
        for y in range(2):
            amount = 64 * x + 16 * y
            rolled = (pltpu.roll(total, amount, 1) if amount else total).astype(BF16)
            for dz in range(3):
                at = 64 * dz + 32 * x + 16 * y
                w2_ref[at : at + 16] = rolled[16 * dz : 16 * dz + 16]
    eye = jnp.where(iota((64, 64), 0) == iota((64, 64), 1), 1.0, 0.0).astype(BF16)
    zero = jnp.zeros((16, 64), BF16)
    for dz in range(3):
        for slot in range(2):
            rows = []
            for dx in range(4):
                for at in range(4):
                    dy = at - slot
                    rows.append(ck_ref[dx, dy, dz] if dx < 3 and 0 <= dy < 3 else zero)
            at = 128 * dz + 64 * slot
            w4_ref[at : at + 64] = dot_t(eye, jnp.concatenate(rows, 0)).astype(BF16)


def returned_kernel(got_ref, w1_ref, own_ref, near_ref, far_ref):
    fil, odd = position()
    before = jnp.maximum(fil - 1, 0)
    after = jnp.minimum(fil + 1, 3)
    for which, msg_ref in enumerate((near_ref, far_ref)):
        for side in range(2):
            at = 18 + 6 * side + 3 * which
            msg_ref[16 + 3 * side : 19 + 3 * side] = got_ref[before, at : at + 3]
            msg_ref[22 + 3 * side : 25 + 3 * side] = got_ref[after, at : at + 3]

        @pl.when(fil == 0)
        def _():
            msg_ref[16:22] = jnp.zeros((6, 16, 128), BF16)

        @pl.when(fil == 3)
        def _():
            msg_ref[22:28] = jnp.zeros((6, 16, 128), BF16)

    w1 = w1_ref[...]
    for pair in range(8):
        window = got_ref[:, 2 * pair : 2 * pair + 4].reshape(256, 128)
        product = dot(w1, window).reshape(2, 3, 3, 16, 128)
        for slot in range(2):
            low, own, high = [
                moved(product[slot, tx, 0], -1) + product[slot, tx, 1] + moved(product[slot, tx, 2], 1) for tx in range(3)
            ]
            own_ref[2 * pair + slot] = own
            near_ref[2 * pair + slot] = jnp.where(odd == 0, high, low).astype(BF16)
            far_ref[2 * pair + slot] = jnp.where(odd == 0, low, high).astype(BF16)


def window_of(refs, start, count):
    return jnp.concatenate([r[pl.ds(start, 4)].reshape(64, r.shape[-1]) for r in refs][:count], 0)


def planes_of(ref):
    return [ref.at[x] for x in range(4)]


def fine_kernel_body(a_ref, b_ref, c_ref, d_ref, ma_ref, mb_ref, mc_ref, md_ref, w2_ref, pooled_ref, mask_ref, all_ref, sums):
    fil, odd = position()
    messages = (ma_ref, mb_ref, mc_ref, md_ref)
    for k, v_ref in enumerate((a_ref, b_ref, c_ref, d_ref)):
        x = k + odd * (3 - 2 * k)
        all_ref[x, 3:35] = v_ref[...]
        for side in range(2):
            lanes = slice(128 * side, 128 * side + 128)
            all_ref[x, 0:3, :, lanes] = messages[k][16 + 3 * side : 19 + 3 * side]
            all_ref[x, 35:38, :, lanes] = messages[k][22 + 3 * side : 25 + 3 * side]

    def block(b):
        window = window_of(planes_of(all_ref), 2 * b, 4)
        product = dot(w2_ref[...], window)
        preact = moved(product[0:64], 1) + product[64:128] + moved(product[128:192], -1)
        act = jnp.maximum(preact, 0.0)
        sums[b] = (act[0:16] + act[16:32]) + (act[32:48] + act[48:64])
        return preact

    block(0)
    block(17)

    def step(b, carry):
        mask_ref[b - 1] = jnp.where(block(b) > 0, 1.0, 0.0).astype(BF16)
        return carry

    lax.fori_loop(1, 17, step, 0, unroll=2)

    @pl.when(fil == 0)
    def _():
        sums[0] = jnp.zeros((16, 256), F32)

    @pl.when(fil == 3)
    def _():
        sums[17] = jnp.zeros((16, 256), F32)

    total = sums[...].reshape(288, 256)
    high = total.astype(BF16)
    low = (total - high.astype(F32)).astype(BF16)
    pool = jnp.where(iota((256, 128), 0) // 2 == iota((256, 128), 1), 0.125, 0.0).astype(BF16)
    pooled_ref[...] = (dot(high, pool) + dot(low, pool)).astype(BF16).reshape(18, 16, 128)


def fine_grad_kernel(own_ref, low_ref, high_ref, all_ref, mask_ref, out_ref, up, acc):
    total = own_ref[...] + (low_ref[0:16].astype(F32) + high_ref[0:16].astype(F32))
    scaled = (total * 0.125).astype(BF16).reshape(256, 128)
    spread = jnp.where(iota((128, 256), 0) == iota((128, 256), 1) // 2, 1.0, 0.0).astype(BF16)
    up[...] = dot(scaled, spread).reshape(16, 16, 256)
    acc[...] = jnp.zeros_like(acc)

    def step(y, carry):
        row = up[y]
        cot = jnp.concatenate([row] * 4, 0) * mask_ref[y].astype(F32)
        left = jnp.concatenate([moved(cot, -1), cot, moved(cot, 1)], 0).astype(BF16)
        window = window_of(planes_of(all_ref), 2 * y + 2, 4)
        acc[...] += dot_t(left, window)
        return carry

    lax.fori_loop(0, 16, step, 0, unroll=2)
    for t in range(3):
        total = None
        for cell in range(4):
            part = roll_left(acc[64 * t + 16 * cell : 64 * t + 16 * cell + 16], 64 * (cell // 2) + 16 * (cell % 2))
            total = part if total is None else total + part
        out_ref[16 * t : 16 * t + 16] = total


def coarse_kernel_body(near_ref, own_ref, far_ref, got_ref, w4_ref, fine_ref, out_ref, grad_ref, rows_out, acc, slab):
    _, odd = position()
    slab[2 - 2 * odd] = near_ref[...]
    slab[1] = own_ref[...]
    slab[2 * odd] = far_ref[...]
    acc[...] = jnp.zeros_like(acc)
    pad = jnp.zeros((64, 128), BF16)

    def step(pair, carry):
        window = jnp.concatenate([window_of([slab.at[x] for x in range(3)], 2 * pair, 3), pad], 0)
        product = dot(w4_ref[...], window)
        result = moved(product[0:128], 1) + product[128:256] + moved(product[256:384], -1)
        rows_out[pl.ds(2 * pair, 2)] = result.astype(BF16).reshape(2, 64, 128)
        cot = jnp.concatenate([got_ref[:, 2 * pair + 1 + s].reshape(64, 128) for s in range(2)], 0).astype(F32)
        left = jnp.concatenate([moved(cot, -1), cot, moved(cot, 1)], 0).astype(BF16)
        acc[...] += dot_t(left, window)
        return carry

    lax.fori_loop(0, 8, step, 0, unroll=2)
    swap = swap_matrix()
    for dest in range(4):
        block = rows_out[:, 16 * dest : 16 * dest + 16, :].reshape(256, 128)
        out_ref[dest] = dot(swap, block).astype(BF16).reshape(16, 16, 128)
    grad_ref[0:48] = fine_ref[...].astype(BF16)
    for t in range(3):
        total = acc[128 * t : 128 * t + 64] + roll_left(acc[128 * t + 64 : 128 * t + 128], 16)
        grad_ref[48 + 64 * t : 112 + 64 * t] = total.astype(BF16)
    grad_ref[240:256] = jnp.zeros((16, 256), BF16)


def sum_kernel(parts_ref, out_ref):
    total = parts_ref[0].astype(F32)
    for src in range(1, 16):
        total = total + parts_ref[src].astype(F32)
    for dest in range(16):
        out_ref[dest] = total.astype(BF16)


def unpack_kernel(grad_ref, got_ref, fine_ref, coarse_ref, out_ref):
    eye = jnp.where(iota((256, 256), 0) == iota((256, 256), 1), 1.0, 0.0).astype(BF16)
    for dz in range(3):
        block = grad_ref[dz].astype(F32)
        columns = dot_t(eye, grad_ref[3 + 4 * dz : 7 + 4 * dz].reshape(64, 256))
        for dx in range(3):
            for dy in range(3):
                at = 64 * dx + 16 * dy
                fine_ref[dx, dy, dz] = roll_left(block, at)[:, 0:16]
                coarse_ref[dx, dy, dz] = columns[at : at + 16]
    for src in range(4):
        out_ref[:, 0, 16 * src : 16 * src + 16, :] = got_ref[src]


def swapped(near, far):
    count = lax.axis_size("vox")
    first = [(i, i ^ 1) for i in range(count)]
    second = [(i, ((i + 1) ^ 1) - 1) for i in range(1, count - 1)]
    return lax.ppermute(near, "vox", first), lax.ppermute(far, "vox", second)


def exchange(pieces, groups):
    return lax.all_to_all(pieces, ("vox", "fil"), 0, 0, tiled=True, axis_index_groups=groups)


def local(volume, fine_kernel, coarse_kernel, coarse_cot):
    plane = ((32, 16, 256), BF16)
    near, far, pay = call(
        pack_kernel,
        [plane, plane, ((4, 30, 16, 128), BF16)],
        scratch=[pltpu.VMEM(volume.shape, BF16), pltpu.VMEM(coarse_cot.shape, BF16), pltpu.SemaphoreType.DMA((2,))],
        n_in=2,
        spec=HBM,
        name="pack",
    )(volume, coarse_cot)
    near_got, far_got = swapped(near, far)
    got = lax.all_to_all(pay, "fil", 0, 0, tiled=True)
    w1, w2, w4 = call(
        weights_kernel, [((288, 256), BF16), ((192, 256), BF16), ((384, 256), BF16)], n_in=2, name="weights"
    )(fine_kernel.transpose(2, 3, 4, 0, 1), coarse_kernel.transpose(2, 3, 4, 1, 0))
    message = ((28, 16, 128), BF16)
    own, near_msg, far_msg = call(
        returned_kernel, [((16, 16, 128), F32), message, message], n_in=2, name="returned"
    )(got, w1)
    near_msg_got, far_msg_got = swapped(near_msg, far_msg)
    pooled, mask, cells = call(
        fine_kernel_body,
        [((18, 16, 128), BF16), ((16, 64, 256), BF16), ((4, 38, 16, 256), BF16)],
        scratch=[pltpu.VMEM((18, 16, 256), F32)],
        n_in=9,
        name="fine",
    )(far_got, far, near, near_got, far_msg_got, far_msg, near_msg, near_msg_got, w2)
    pooled_near, pooled_far = swapped(pooled, pooled)
    (fine_part,) = call(
        fine_grad_kernel,
        [((48, 256), F32)],
        scratch=[pltpu.VMEM((16, 16, 256), F32), pltpu.VMEM((192, 256), F32)],
        n_in=5,
        name="fine_grad",
    )(own, near_msg_got, far_msg_got, cells, mask)
    out_pieces, grads = call(
        coarse_kernel_body,
        [((4, 16, 16, 128), BF16), ((256, 256), BF16)],
        scratch=[pltpu.VMEM((16, 64, 128), BF16), pltpu.VMEM((384, 256), F32), pltpu.VMEM((3, 18, 16, 128), BF16)],
        n_in=6,
        name="coarse",
    )(pooled_near, pooled, pooled_far, got, w4, fine_part)
    out_got = lax.all_to_all(out_pieces, "fil", 0, 0, tiled=True)
    lines = [[16 * g + j for j in range(16)] for g in range(16)]
    sheets = [[16 * g + j for g in range(16)] for j in range(16)]
    summed = call(sum_kernel, [((16, 16, 256), BF16)], name="sum")
    parts = exchange(grads.reshape(16, 16, 256), lines)
    parts = exchange(summed(parts)[0], sheets)
    spread = exchange(summed(parts)[0], lines)
    grad_fine, grad_coarse, coarse_out = call(
        unpack_kernel,
        [((3, 3, 3, 16, 16), F32), ((3, 3, 3, 16, 64), F32), ((16, 1, 64, 128), BF16)],
        n_in=2,
        name="unpack",
    )(spread, out_got)
    return (coarse_out, grad_fine.transpose(3, 4, 0, 1, 2), grad_coarse.transpose(4, 3, 0, 1, 2))


def solution(mesh):
    in_specs = (P(None, "vox", "fil", None), P(), P(), P("fil", "vox", None, None))
    out_specs = (P("fil", "vox", None, None), P(), P())
    return jax.shard_map(local, mesh=mesh, in_specs=in_specs, out_specs=out_specs, check_vma=False)
```

profile of v0, /device:TPU:1, one launch (start us, length us, event | category | flops | bytes accessed | tf_op | source)
XLA Modules:
  0.0 107.2 jit_solution(15329554110750598103)
XLA Ops:
  0.6 1.0 copy-done
  1.7 0.9 copy-done.1
  2.6 1.5 %pack.1 = (bf16[32,16,256]{2,1,0:T(8,128)(2,1)S(1)}, bf16[32,16,256]{2,1,0:T(8,128)(2,1)S(1)}, bf16[4,30,16,128]{3,2,1,0:T(8,128)(2,1)}) custom-call(bf16[16,2,32,256]{3,2,1,0:T(8,128)(2,1)S(1)} %copy-done, bf16[16,1,64,128]{3,2,1,0:T(8,128)(2,1)S(1)} %copy-done.1), custom_call_target="tpu_custom_call" | custom-call | flops 2000000000 | bytes 1000000 | tf_op jit(solution)/shard_map/pack/pallas_call | solution.py:309
  4.1 6.6 %all-to-all-start = ((bf16[4,30,16,128]{3,2,1,0:T(8,128)(2,1)}), bf16[4,30,16,128]{3,2,1,0:T(8,128)(2,1)S(1)}, u32[]{:S(2)}, u32[]{:S(2)}) async-start(bf16[4,30,16,128]{3,2,1,0:T(8,128)(2,1)} %get-tuple-element.22), calls=%async_computation | async-start | bytes 983040 | tf_op jit(solution)/shard_map/all_to_all | solution.py:318
  10.8 0.7 collective-permute-start
  11.4 6.8 %collective-permute-start.1 = (bf16[32,16,256]{2,1,0:T(8,128)(2,1)S(1)}, bf16[32,16,256]{2,1,0:T(8,128)(2,1)S(1)}, u32[]{:S(2)}, u32[]{:S(2)}) collective-permute-start(bf16[32,16,256]{2,1,0:T(8,128)(2,1)S(1)} %get-tuple-element.21.c_ref), channel_id=1, source_target_pairs={{0,4},{4,0},{8,12},{12,8},{16,20},{20,16},{24,28},{28,24},{32,36},... | collective-permute-start | bytes 786440 | tf_op jit(solution)/shard_map/ppermute | solution.py:300
  18.2 0.5 weights.1
  18.7 0.0 all-to-all-done.got_ref
  18.8 0.6 returned.1
  19.3 0.7 collective-permute-start.2
  20.0 9.7 %collective-permute-start.3 = (bf16[28,16,128]{2,1,0:T(8,128)(2,1)S(1)}, bf16[28,16,128]{2,1,0:T(8,128)(2,1)S(1)}, u32[]{:S(2)}, u32[]{:S(2)}) collective-permute-start(bf16[28,16,128]{2,1,0:T(8,128)(2,1)S(1)} %get-tuple-element.25.mc_ref), channel_id=1, source_target_pairs={{0,4},{4,0},{8,12},{12,8},{16,20},{20,16},{24,28},{28,24},{32,36},... | collective-permute-start | bytes 344072 | tf_op jit(solution)/shard_map/ppermute | solution.py:300
  29.7 0.0 collective-permute-done.1.d_ref
  29.8 6.1 %collective-permute-done.3.md_ref.low_ref = bf16[28,16,128]{2,1,0:T(8,128)(2,1)S(1)} collective-permute-done((bf16[28,16,128]{2,1,0:T(8,128)(2,1)S(1)}, bf16[28,16,128]{2,1,0:T(8,128)(2,1)S(1)}, u32[]{:S(2)}, u32[]{:S(2)}) %collective-permute-start.3) | collective-permute-done | bytes 114720 | tf_op jit(solution)/shard_map/ppermute | solution.py:300
  35.9 3.1 %fine.1 = (bf16[18,16,128]{2,1,0:T(8,128)(2,1)S(1)}, bf16[16,64,256]{2,1,0:T(8,128)(2,1)S(1)}, bf16[4,38,16,256]{3,2,1,0:T(8,128)(2,1)S(1)}) custom-call(bf16[32,16,256]{2,1,0:T(8,128)(2,1)S(1)} %collective-permute-done.a_ref, bf16[32,16,256]{2,1,0:T(8,128)(2,1)S(1)} %get-tuple-element.20.b_ref, bf16[32,16,256]{2,1,0:T(8,128)(2,1)S(1)} %get-tuple-element.21.c_ref, ...), custom_call_target="tpu_custom_call" | custom-call | flops 2000000000 | bytes 1000000 | tf_op jit(solution)/shard_map/fine/pallas_call | solution.py:327
  39.0 0.7 collective-permute-start.5
  39.7 2.5 %collective-permute-start.4 = (bf16[18,16,128]{2,1,0:T(8,128)(2,1)S(1)}, bf16[18,16,128]{2,1,0:T(8,128)(2,1)S(1)}, u32[]{:S(2)}, u32[]{:S(2)}) collective-permute-start(bf16[18,16,128]{2,1,0:T(8,128)(2,1)S(1)} %get-tuple-element.27.own_ref), channel_id=1, source_target_pairs={{0,4},{4,0},{8,12},{12,8},{16,20},{20,16},{24,28},{28,24},{32,36},... | collective-permute-start | bytes 221192 | tf_op jit(solution)/shard_map/ppermute | solution.py:300
  42.2 2.4 %fine_grad.1.fine_ref = f32[48,256]{1,0:T(8,128)S(1)} custom-call(f32[16,16,128]{2,1,0:T(8,128)S(1)} %get-tuple-element.29.own_ref, bf16[28,16,128]{2,1,0:T(8,128)(2,1)S(1)} %collective-permute-done.3.md_ref.low_ref, bf16[28,16,128]{2,1,0:T(8,128)(2,1)S(1)} %collective-permute-done.2.ma_ref.high_ref, bf16[4,38,16,256]{3,2,1,0:T(8,128)(2,1)S(1)} %get-tuple-element.30.all_ref, ...), custom_call_target="tpu_custom_call" | custom-call | flops 2000000000 | bytes 1000000 | tf_op jit(solution)/shard_map/fine_grad/pallas_call | solution.py:335
  44.6 2.7 %coarse.1 = (bf16[4,16,16,128]{3,2,1,0:T(8,128)(2,1)}, bf16[256,256]{1,0:T(8,128)(2,1)S(1)}) custom-call(bf16[18,16,128]{2,1,0:T(8,128)(2,1)S(1)} %collective-permute-done.4.near_ref, bf16[18,16,128]{2,1,0:T(8,128)(2,1)S(1)} %get-tuple-element.27.own_ref, bf16[18,16,128]{2,1,0:T(8,128)(2,1)S(1)} %collective-permute-done.5.far_ref, ...), custom_call_target="tpu_custom_call" | custom-call | flops 2000000000 | bytes 1000000 | tf_op jit(solution)/shard_map/coarse/pallas_call | solution.py:342
  47.3 19.4 %all_to_all.25.parts_ref = bf16[16,16,256]{2,1,0:T(8,128)(2,1)S(1)} all-to-all(bf16[16,16,256]{2,1,0:T(8,128)(2,1)S(1)} %bitcast.5), channel_id=1, replica_groups={{0,1,2,3,4,5,6,7,8,9,10,11,12,13,14,15},{16,17,18,19,20,21,22,23,24,25,..., dimensions={0} | all-to-all | bytes 262144 | tf_op jit(solution)/shard_map/all_to_all | solution.py:304
  66.7 17.2 %all_to_all.26.parts_ref = bf16[16,16,256]{2,1,0:T(8,128)(2,1)S(1)} all-to-all(bf16[16,16,256]{2,1,0:T(8,128)(2,1)S(1)} %sum.2), channel_id=1, replica_groups={{0,16,32,48,64,80,96,112,128,144,160,176,192,208,224,240},{1,17,33,49,6..., dimensions={0} | all-to-all | bytes 262144 | tf_op jit(solution)/shard_map/all_to_all | solution.py:304
  83.9 4.7 %all-to-all-start.4 = ((bf16[4,16,16,128]{3,2,1,0:T(8,128)(2,1)}), bf16[4,16,16,128]{3,2,1,0:T(8,128)(2,1)S(1)}, u32[]{:S(2)}, u32[]{:S(2)}) async-start(bf16[4,16,16,128]{3,2,1,0:T(8,128)(2,1)} %get-tuple-element.33), calls=%async_computation.4 | async-start | bytes 524288 | tf_op jit(solution)/shard_map/all_to_all | solution.py:349
  88.6 5.0 %all-to-all-done.4.got_ref = bf16[4,16,16,128]{3,2,1,0:T(8,128)(2,1)S(1)} async-done(((bf16[4,16,16,128]{3,2,1,0:T(8,128)(2,1)}), bf16[4,16,16,128]{3,2,1,0:T(8,128)(2,1)S(1)}, u32[]{:S(2)}, u32[]{:S(2)}) %all-to-all-start.4) | async-done | bytes 262176 | tf_op jit(solution)/shard_map/all_to_all | solution.py:349
  93.6 12.5 %all_to_all.27.grad_ref = bf16[16,16,256]{2,1,0:T(8,128)(2,1)S(1)} all-to-all(bf16[16,16,256]{2,1,0:T(8,128)(2,1)S(1)} %sum.3), channel_id=1, replica_groups={{0,1,2,3,4,5,6,7,8,9,10,11,12,13,14,15},{16,17,18,19,20,21,22,23,24,25,..., dimensions={0} | all-to-all | bytes 262144 | tf_op jit(solution)/shard_map/all_to_all | solution.py:304
  106.1 1.0 unpack.1
  (12 shorter events, 0.1 us)
Async XLA Ops:
  0.6 1.0 copy-start
  1.7 0.9 copy-start.1
  2.6 15.6 %copy-start.2 = (bf16[16,16,3,3,3]{1,0,4,3,2:T(8,128)(2,1)S(1)}, bf16[16,16,3,3,3]{1,0,4,3,2:T(8,128)(2,1)}, u32[]{:S(2)}) copy-start(bf16[16,16,3,3,3]{1,0,4,3,2:T(8,128)(2,1)} %param.5) | copy-start | bytes 41476
  2.6 15.6 %copy-start.3 = (bf16[64,16,3,3,3]{0,1,4,3,2:T(8,128)(2,1)S(1)}, bf16[64,16,3,3,3]{0,1,4,3,2:T(8,128)(2,1)}, u32[]{:S(2)}) copy-start(bf16[64,16,3,3,3]{0,1,4,3,2:T(8,128)(2,1)} %param.6) | copy-start | bytes 165892
  4.1 14.6 %all-to-all-start = ((bf16[4,30,16,128]{3,2,1,0:T(8,128)(2,1)}), bf16[4,30,16,128]{3,2,1,0:T(8,128)(2,1)S(1)}, u32[]{:S(2)}, u32[]{:S(2)}) async-start(bf16[4,30,16,128]{3,2,1,0:T(8,128)(2,1)} %get-tuple-element.22), calls=%async_computation | async-start | bytes 983040 | tf_op jit(solution)/shard_map/all_to_all | solution.py:318
  10.8 19.0 %collective-permute-start = (bf16[32,16,256]{2,1,0:T(8,128)(2,1)S(1)}, bf16[32,16,256]{2,1,0:T(8,128)(2,1)S(1)}, u32[]{:S(2)}, u32[]{:S(2)}) collective-permute-start(bf16[32,16,256]{2,1,0:T(8,128)(2,1)S(1)} %get-tuple-element.20.b_ref), channel_id=1, source_target_pairs={{4,8},{8,4},{12,16},{16,12},{20,24},{24,20},{28,32},{32,28},{36,40... | collective-permute-start | bytes 786440 | tf_op jit(solution)/shard_map/ppermute | solution.py:300
  11.4 18.3 %collective-permute-start.1 = (bf16[32,16,256]{2,1,0:T(8,128)(2,1)S(1)}, bf16[32,16,256]{2,1,0:T(8,128)(2,1)S(1)}, u32[]{:S(2)}, u32[]{:S(2)}) collective-permute-start(bf16[32,16,256]{2,1,0:T(8,128)(2,1)S(1)} %get-tuple-element.21.c_ref), channel_id=1, source_target_pairs={{0,4},{4,0},{8,12},{12,8},{16,20},{20,16},{24,28},{28,24},{32,36},... | collective-permute-start | bytes 786440 | tf_op jit(solution)/shard_map/ppermute | solution.py:300
  19.3 10.4 %collective-permute-start.2 = (bf16[28,16,128]{2,1,0:T(8,128)(2,1)S(1)}, bf16[28,16,128]{2,1,0:T(8,128)(2,1)S(1)}, u32[]{:S(2)}, u32[]{:S(2)}) collective-permute-start(bf16[28,16,128]{2,1,0:T(8,128)(2,1)S(1)} %get-tuple-element.24.mb_ref), channel_id=1, source_target_pairs={{4,8},{8,4},{12,16},{16,12},{20,24},{24,20},{28,32},{32,28},{36,40... | collective-permute-start | bytes 344072 | tf_op jit(solution)/shard_map/ppermute | solution.py:300
  20.0 15.9 %collective-permute-start.3 = (bf16[28,16,128]{2,1,0:T(8,128)(2,1)S(1)}, bf16[28,16,128]{2,1,0:T(8,128)(2,1)S(1)}, u32[]{:S(2)}, u32[]{:S(2)}) collective-permute-start(bf16[28,16,128]{2,1,0:T(8,128)(2,1)S(1)} %get-tuple-element.25.mc_ref), channel_id=1, source_target_pairs={{0,4},{4,0},{8,12},{12,8},{16,20},{20,16},{24,28},{28,24},{32,36},... | collective-permute-start | bytes 344072 | tf_op jit(solution)/shard_map/ppermute | solution.py:300
  39.0 5.5 %collective-permute-start.5 = (bf16[18,16,128]{2,1,0:T(8,128)(2,1)S(1)}, bf16[18,16,128]{2,1,0:T(8,128)(2,1)S(1)}, u32[]{:S(2)}, u32[]{:S(2)}) collective-permute-start(bf16[18,16,128]{2,1,0:T(8,128)(2,1)S(1)} %get-tuple-element.27.own_ref), channel_id=1, source_target_pairs={{4,8},{8,4},{12,16},{16,12},{20,24},{24,20},{28,32},{32,28},{36,40... | collective-permute-start | bytes 221192 | tf_op jit(solution)/shard_map/ppermute | solution.py:300
  39.7 4.9 %collective-permute-start.4 = (bf16[18,16,128]{2,1,0:T(8,128)(2,1)S(1)}, bf16[18,16,128]{2,1,0:T(8,128)(2,1)S(1)}, u32[]{:S(2)}, u32[]{:S(2)}) collective-permute-start(bf16[18,16,128]{2,1,0:T(8,128)(2,1)S(1)} %get-tuple-element.27.own_ref), channel_id=1, source_target_pairs={{0,4},{4,0},{8,12},{12,8},{16,20},{20,16},{24,28},{28,24},{32,36},... | collective-permute-start | bytes 221192 | tf_op jit(solution)/shard_map/ppermute | solution.py:300
  83.9 9.8 %all-to-all-start.4 = ((bf16[4,16,16,128]{3,2,1,0:T(8,128)(2,1)}), bf16[4,16,16,128]{3,2,1,0:T(8,128)(2,1)S(1)}, u32[]{:S(2)}, u32[]{:S(2)}) async-start(bf16[4,16,16,128]{3,2,1,0:T(8,128)(2,1)} %get-tuple-element.33), calls=%async_computation.4 | async-start | bytes 524288 | tf_op jit(solution)/shard_map/all_to_all | solution.py:349
where the time goes:
time: 108 us; the launch traced here: 107 us
  blocking collectives  49.1 us (45%)
  starting transfers between devices  32.4 us (30%)
  Pallas kernels  11.8 us (11%)
  waiting for transfers between devices  11.2 us (10%)
  local copies, waits for them, and re-layouts  1.99 us (2%)
    all_to_all x3, blocking collectives, exchange(): lax.all_to_all(pieces, ('vox', 'fil'), 0, 0, tiled=True, axis_index_group...  49.1 us
    ppermute x6, starting transfers between devices, swapped(): return (lax.ppermute(near, 'vox', first), lax.ppermute(far, 'vox', second))  21 us
    all_to_all x1, starting transfers between devices, local(): got = lax.all_to_all(pay, 'fil', 0, 0, tiled=True)  6.65 us
    ppermute x6, waiting for transfers between devices, swapped(): return (lax.ppermute(near, 'vox', first), lax.ppermute(far, 'vox', second))  6.15 us
    all_to_all x1, waiting for transfers between devices, local(): out_got = lax.all_to_all(out_pieces, 'fil', 0, 0, tiled=True)  5.01 us
    all_to_all x1, starting transfers between devices, local(): out_got = lax.all_to_all(out_pieces, 'fil', 0, 0, tiled=True)  4.72 us
    pallas_call x1, Pallas kernels, local(): call(fine_kernel_body, [((18, 16, 128), BF16), ((16, 64, 256), BF16), ((4...  3.1 us
    pallas_call x1, Pallas kernels, local(): call(coarse_kernel_body, [((4, 16, 16, 128), BF16), ((256, 256), BF16)],...  2.71 us
  transfers between devices with their start and end apart: 8, of which 2 were waited for; matrix products, arithmetic and copies ran while one was open for 0% of the time, Pallas kernels for 3%

commit v1 on v0

--- a/solution.py
+++ b/solution.py
@@ -47,7 +47,7 @@
     return jnp.where(iota(x.shape, 1) == edge, 0.0, pltpu.roll(x, step % width, 1))
 
 
-def call(body, outs, scratch=(), flops=2_000_000_000, n_in=1, spec=VMEM, name=None):
+def call(body, outs, scratch=(), flops=2_000_000_000, n_in=1, spec=VMEM, vmem=32 * 1024 * 1024, name=None):
     specs = [spec] * n_in
     return pl.pallas_call(
         body,
@@ -56,7 +56,7 @@
         out_specs=tuple(VMEM for _ in outs),
         scratch_shapes=scratch,
         cost_estimate=pl.CostEstimate(flops=flops, bytes_accessed=1_000_000, transcendentals=0),
-        compiler_params=pltpu.CompilerParams(vmem_limit_bytes=32 * 1024 * 1024),
+        compiler_params=pltpu.CompilerParams(vmem_limit_bytes=vmem),
         name=name,
     )
 
@@ -200,7 +200,7 @@
         mask_ref[b - 1] = jnp.where(block(b) > 0, 1.0, 0.0).astype(BF16)
         return carry
 
-    lax.fori_loop(1, 17, step, 0, unroll=2)
+    lax.fori_loop(1, 17, step, 0, unroll=True)
 
     @pl.when(fil == 0)
     def _():
@@ -232,7 +232,7 @@
         acc[...] += dot_t(left, window)
         return carry
 
-    lax.fori_loop(0, 16, step, 0, unroll=2)
+    lax.fori_loop(0, 16, step, 0, unroll=True)
     for t in range(3):
         total = None
         for cell in range(4):
@@ -241,8 +241,8 @@
         out_ref[16 * t : 16 * t + 16] = total
 
 
-def coarse_kernel_body(near_ref, own_ref, far_ref, got_ref, w4_ref, fine_ref, out_ref, grad_ref, rows_out, acc, slab):
-    _, odd = position()
+def coarse_kernel_body(near_ref, own_ref, far_ref, got_ref, w4_ref, fine_ref, out0_ref, out1_ref, out2_ref, out3_ref, grad_ref, rows_out, acc, slab):
+    fil, odd = position()
     slab[2 - 2 * odd] = near_ref[...]
     slab[1] = own_ref[...]
     slab[2 * odd] = far_ref[...]
@@ -253,17 +253,19 @@
         window = jnp.concatenate([window_of([slab.at[x] for x in range(3)], 2 * pair, 3), pad], 0)
         product = dot(w4_ref[...], window)
         result = moved(product[0:128], 1) + product[128:256] + moved(product[256:384], -1)
-        rows_out[pl.ds(2 * pair, 2)] = result.astype(BF16).reshape(2, 64, 128)
+        result = result.astype(BF16).reshape(2, 4, 16, 128)
+        for dest in range(4):
+            rows_out[dest, pl.ds(2 * pair, 2)] = result[:, dest]
         cot = jnp.concatenate([got_ref[:, 2 * pair + 1 + s].reshape(64, 128) for s in range(2)], 0).astype(F32)
         left = jnp.concatenate([moved(cot, -1), cot, moved(cot, 1)], 0).astype(BF16)
         acc[...] += dot_t(left, window)
         return carry
 
-    lax.fori_loop(0, 8, step, 0, unroll=2)
+    lax.fori_loop(0, 8, step, 0, unroll=True)
     swap = swap_matrix()
-    for dest in range(4):
-        block = rows_out[:, 16 * dest : 16 * dest + 16, :].reshape(256, 128)
-        out_ref[dest] = dot(swap, block).astype(BF16).reshape(16, 16, 128)
+    for k, out_ref in enumerate((out0_ref, out1_ref, out2_ref, out3_ref)):
+        block = rows_out[lax.bitwise_xor(fil, k)].reshape(256, 128)
+        out_ref[...] = dot(swap, block).astype(BF16).reshape(16, 16, 128)
     grad_ref[0:48] = fine_ref[...].astype(BF16)
     for t in range(3):
         total = acc[128 * t : 128 * t + 64] + roll_left(acc[128 * t + 64 : 128 * t + 128], 16)
@@ -279,7 +281,8 @@
         out_ref[dest] = total.astype(BF16)
 
 
-def unpack_kernel(grad_ref, got_ref, fine_ref, coarse_ref, out_ref):
+def unpack_kernel(grad_ref, got0_ref, got1_ref, got2_ref, got3_ref, fine_ref, coarse_ref, out_ref):
+    fil, _ = position()
     eye = jnp.where(iota((256, 256), 0) == iota((256, 256), 1), 1.0, 0.0).astype(BF16)
     for dz in range(3):
         block = grad_ref[dz].astype(F32)
@@ -289,8 +292,9 @@
                 at = 64 * dx + 16 * dy
                 fine_ref[dx, dy, dz] = roll_left(block, at)[:, 0:16]
                 coarse_ref[dx, dy, dz] = columns[at : at + 16]
-    for src in range(4):
-        out_ref[:, 0, 16 * src : 16 * src + 16, :] = got_ref[src]
+    for k, got_ref in enumerate((got0_ref, got1_ref, got2_ref, got3_ref)):
+        at = pl.multiple_of(16 * lax.bitwise_xor(fil, k), 16)
+        out_ref[:, 0, pl.ds(at, 16), :] = got_ref[...]
 
 
 def swapped(near, far):
@@ -312,6 +316,7 @@
         scratch=[pltpu.VMEM(volume.shape, BF16), pltpu.VMEM(coarse_cot.shape, BF16), pltpu.SemaphoreType.DMA((2,))],
         n_in=2,
         spec=HBM,
+        vmem=63 * 1024 * 1024,
         name="pack",
     )(volume, coarse_cot)
     near_got, far_got = swapped(near, far)
@@ -339,14 +344,16 @@
         n_in=5,
         name="fine_grad",
     )(own, near_msg_got, far_msg_got, cells, mask)
-    out_pieces, grads = call(
+    *out_pieces, grads = call(
         coarse_kernel_body,
-        [((4, 16, 16, 128), BF16), ((256, 256), BF16)],
-        scratch=[pltpu.VMEM((16, 64, 128), BF16), pltpu.VMEM((384, 256), F32), pltpu.VMEM((3, 18, 16, 128), BF16)],
+        [((16, 16, 128), BF16)] * 4 + [((256, 256), BF16)],
+        scratch=[pltpu.VMEM((4, 16, 16, 128), BF16), pltpu.VMEM((384, 256), F32), pltpu.VMEM((3, 18, 16, 128), BF16)],
         n_in=6,
         name="coarse",
     )(pooled_near, pooled, pooled_far, got, w4, fine_part)
-    out_got = lax.all_to_all(out_pieces, "fil", 0, 0, tiled=True)
+    out_got = out_pieces[:1] + [
+        lax.ppermute(out_pieces[k], "fil", [(i, i ^ k) for i in range(4)]) for k in range(1, 4)
+    ]
     lines = [[16 * g + j for j in range(16)] for g in range(16)]
     sheets = [[16 * g + j for g in range(16)] for j in range(16)]
     summed = call(sum_kernel, [((16, 16, 256), BF16)], name="sum")
@@ -356,9 +363,9 @@
     grad_fine, grad_coarse, coarse_out = call(
         unpack_kernel,
         [((3, 3, 3, 16, 16), F32), ((3, 3, 3, 16, 64), F32), ((16, 1, 64, 128), BF16)],
-        n_in=2,
+        n_in=5,
         name="unpack",
-    )(spread, out_got)
+    )(spread, *out_got)
     return (coarse_out, grad_fine.transpose(3, 4, 0, 1, 2), grad_coarse.transpose(4, 3, 0, 1, 2))
 
 

time: 108 us -> 95.9 us (0.89)
  blocking collectives: 49.1 us -> 38 us
  Pallas kernels: 11.8 us -> 8.98 us
  starting transfers between devices: 32.4 us -> 34.9 us
  local copies, waits for them, and re-layouts: 1.99 us -> 0.02 us
  waiting for transfers between devices: 11.2 us -> 12.9 us
    all_to_all x3 -> x2, blocking collectives: 49.1 us -> 38 us  [exchange(): lax.all_to_all(pieces, ('vox', 'fil'), 0, 0, tiled=True, axis_index_group...]
    ppermute x0 -> x3, waiting for transfers between devices: none -> 6.29 us  [local(): lax.ppermute(out_pieces[k], 'fil', [(i, i ^ k) for i in range(4)])]
    all_to_all x1, waiting for transfers between devices: 5.01 us -> 0.97 us  [exchange(): lax.all_to_all(pieces, ('vox', 'fil'), 0, 0, tiled=True, axis_index_group...]
    ppermute x0 -> x3, starting transfers between devices: none -> 2.14 us  [local(): lax.ppermute(out_pieces[k], 'fil', [(i, i ^ k) for i in range(4)])]
    unnamed x8, local copies, waits for them, and re-layouts: 1.99 us -> 0.02 us
    pallas_call x1, Pallas kernels: 3.1 us -> 1.3 us  [local(): call(fine_kernel_body, [((18, 16, 128), BF16), ((16, 64, 256), BF16), ((4...]
    pallas_call x1, Pallas kernels: 2.71 us -> 1.35 us  [local(): call(coarse_kernel_body, [((16, 16, 128), BF16)] * 4 + [((256, 256), BF16...]
    pallas_call x1, Pallas kernels: 2.36 us -> 1.04 us  [local(): call(fine_grad_kernel, [((48, 256), F32)], scratch=[pltpu.VMEM((16, 16, 2...]
  transfers between devices with their start and end apart: 8 -> 11, of which waited for: 2 -> 6; matrix products, arithmetic and copies ran while one was open for 0% -> 0% of each run, Pallas kernels for 3% -> 2%
where the time goes in v1:
time: 95.9 us; the launch traced here: 95.6 us
  blocking collectives  38 us (40%)
  starting transfers between devices  34.9 us (36%)
  waiting for transfers between devices  12.9 us (13%)
  Pallas kernels  8.98 us (9%)
    all_to_all x2, blocking collectives, exchange(): lax.all_to_all(pieces, ('vox', 'fil'), 0, 0, tiled=True, axis_index_group...  38 us
    ppermute x6, starting transfers between devices, swapped(): return (lax.ppermute(near, 'vox', first), lax.ppermute(far, 'vox', second))  21.5 us
    all_to_all x1, starting transfers between devices, local(): got = lax.all_to_all(pay, 'fil', 0, 0, tiled=True)  6.65 us
    ppermute x3, waiting for transfers between devices, local(): lax.ppermute(out_pieces[k], 'fil', [(i, i ^ k) for i in range(4)])  6.29 us
    ppermute x6, waiting for transfers between devices, swapped(): return (lax.ppermute(near, 'vox', first), lax.ppermute(far, 'vox', second))  5.67 us
    all_to_all x1, starting transfers between devices, exchange(): lax.all_to_all(pieces, ('vox', 'fil'), 0, 0, tiled=True, axis_index_group...  4.65 us
    pallas_call x1, Pallas kernels, local(): call(pack_kernel, [plane, plane, ((4, 30, 16, 128), BF16)], scratch=[pltp...  2.47 us
    ppermute x3, starting transfers between devices, local(): lax.ppermute(out_pieces[k], 'fil', [(i, i ^ k) for i in range(4)])  2.14 us
  transfers between devices with their start and end apart: 11, of which 6 were waited for; matrix products, arithmetic and copies ran while one was open for 0% of the time, Pallas kernels for 2%

profile of v1, /device:TPU:1, one launch (start us, length us, event | category | flops | bytes accessed | tf_op | source)
XLA Modules:
  0.0 95.6 jit_solution(12458711816159064798)
XLA Ops:
  0.7 2.5 %pack.1 = (bf16[32,16,256]{2,1,0:T(8,128)(2,1)}, bf16[32,16,256]{2,1,0:T(8,128)(2,1)}, bf16[4,30,16,128]{3,2,1,0:T(8,128)(2,1)}) custom-call(bf16[16,2,32,256]{3,2,1,0:T(8,128)(2,1)} %vol_hbm.1, bf16[16,1,64,128]{3,2,1,0:T(8,128)(2,1)} %cot_hbm.1), custom_call_target="tpu_custom_call" | custom-call | flops 2000000000 | bytes 1000000 | tf_op jit(solution)/shard_map/pack/pallas_call | solution.py:313
  3.1 6.6 %all-to-all-start = ((bf16[4,30,16,128]{3,2,1,0:T(8,128)(2,1)}), bf16[4,30,16,128]{3,2,1,0:T(8,128)(2,1)S(1)}, u32[]{:S(2)}, u32[]{:S(2)}) async-start(bf16[4,30,16,128]{3,2,1,0:T(8,128)(2,1)} %get-tuple-element.25), calls=%async_computation | async-start | bytes 983040 | tf_op jit(solution)/shard_map/all_to_all | solution.py:323
  9.8 0.7 collective-permute-start
  10.4 6.8 %collective-permute-start.1 = (bf16[32,16,256]{2,1,0:T(8,128)(2,1)}, bf16[32,16,256]{2,1,0:T(8,128)(2,1)S(1)}, u32[]{:S(2)}, u32[]{:S(2)}) collective-permute-start(bf16[32,16,256]{2,1,0:T(8,128)(2,1)} %get-tuple-element.24.c_ref), channel_id=1, source_target_pairs={{0,4},{4,0},{8,12},{12,8},{16,20},{20,16},{24,28},{28,24},{32,36},... | collective-permute-start | bytes 786440 | tf_op jit(solution)/shard_map/ppermute | solution.py:304
  17.8 0.6 returned.1
  18.4 0.7 collective-permute-start.2
  19.0 9.5 %collective-permute-start.3 = (bf16[28,16,128]{2,1,0:T(8,128)(2,1)S(1)}, bf16[28,16,128]{2,1,0:T(8,128)(2,1)S(1)}, u32[]{:S(2)}, u32[]{:S(2)}) collective-permute-start(bf16[28,16,128]{2,1,0:T(8,128)(2,1)S(1)} %get-tuple-element.28.mc_ref), channel_id=1, source_target_pairs={{0,4},{4,0},{8,12},{12,8},{16,20},{20,16},{24,28},{28,24},{32,36},... | collective-permute-start | bytes 344072 | tf_op jit(solution)/shard_map/ppermute | solution.py:304
  28.5 1.1 %collective-permute-done.1.d_ref = bf16[32,16,256]{2,1,0:T(8,128)(2,1)S(1)} collective-permute-done((bf16[32,16,256]{2,1,0:T(8,128)(2,1)}, bf16[32,16,256]{2,1,0:T(8,128)(2,1)S(1)}, u32[]{:S(2)}, u32[]{:S(2)}) %collective-permute-start.1) | collective-permute-done | bytes 262176 | tf_op jit(solution)/shard_map/ppermute | solution.py:304
  29.6 3.9 %collective-permute-done.3.md_ref.low_ref = bf16[28,16,128]{2,1,0:T(8,128)(2,1)S(1)} collective-permute-done((bf16[28,16,128]{2,1,0:T(8,128)(2,1)S(1)}, bf16[28,16,128]{2,1,0:T(8,128)(2,1)S(1)}, u32[]{:S(2)}, u32[]{:S(2)}) %collective-permute-start.3) | collective-permute-done | bytes 114720 | tf_op jit(solution)/shard_map/ppermute | solution.py:304
  33.5 1.3 %fine.1 = (bf16[18,16,128]{2,1,0:T(8,128)(2,1)S(1)}, bf16[16,64,256]{2,1,0:T(8,128)(2,1)S(1)}, bf16[4,38,16,256]{3,2,1,0:T(8,128)(2,1)S(1)}) custom-call(bf16[32,16,256]{2,1,0:T(8,128)(2,1)S(1)} %collective-permute-done.a_ref, bf16[32,16,256]{2,1,0:T(8,128)(2,1)S(1)} %copy-done.1, bf16[32,16,256]{2,1,0:T(8,128)(2,1)S(1)} %copy-done, ...), custom_call_target="tpu_custom_call" | custom-call | flops 2000000000 | bytes 1000000 | tf_op jit(solution)/shard_map/fine/pallas_call | solution.py:332
  34.8 0.7 collective-permute-start.5
  35.5 3.2 %collective-permute-start.4 = (bf16[18,16,128]{2,1,0:T(8,128)(2,1)S(1)}, bf16[18,16,128]{2,1,0:T(8,128)(2,1)S(1)}, u32[]{:S(2)}, u32[]{:S(2)}) collective-permute-start(bf16[18,16,128]{2,1,0:T(8,128)(2,1)S(1)} %get-tuple-element.30.own_ref), channel_id=1, source_target_pairs={{0,4},{4,0},{8,12},{12,8},{16,20},{20,16},{24,28},{28,24},{32,36},... | collective-permute-start | bytes 221192 | tf_op jit(solution)/shard_map/ppermute | solution.py:304
  38.7 1.0 %fine_grad.1.fine_ref = f32[48,256]{1,0:T(8,128)S(1)} custom-call(f32[16,16,128]{2,1,0:T(8,128)S(1)} %get-tuple-element.32.own_ref, bf16[28,16,128]{2,1,0:T(8,128)(2,1)S(1)} %collective-permute-done.3.md_ref.low_ref, bf16[28,16,128]{2,1,0:T(8,128)(2,1)S(1)} %collective-permute-done.2.ma_ref.high_ref, bf16[4,38,16,256]{3,2,1,0:T(8,128)(2,1)S(1)} %get-tuple-element.33.all_ref, ...), custom_call_target="tpu_custom_call" | custom-call | flops 2000000000 | bytes 1000000 | tf_op jit(solution)/shard_map/fine_grad/pallas_call | solution.py:340
  39.7 0.7 collective-permute-done.4.near_ref
  40.4 1.4 %coarse.1 = (bf16[16,16,128]{2,1,0:T(8,128)(2,1)S(1)}, bf16[16,16,128]{2,1,0:T(8,128)(2,1)S(1)}, bf16[16,16,128]{2,1,0:T(8,128)(2,1)S(1)}, bf16[16,16,128]{2,1,0:T(8,128)(2,1)S(1)}, bf16[256,256]{1,0:T(8,128)(2,1)S(1)}) custom-call(bf16[18,16,128]{2,1,0:T(8,128)(2,1)S(1)} %collective-permute-done.4.near_ref, ...), custom_call_target="tpu_custom_call" | custom-call | flops 2000000000 | bytes 1000000 | tf_op jit(solution)/shard_map/coarse/pallas_call | solution.py:347
  41.8 20.7 %all_to_all.20.parts_ref = bf16[16,16,256]{2,1,0:T(8,128)(2,1)S(1)} all-to-all(bf16[16,16,256]{2,1,0:T(8,128)(2,1)S(1)} %bitcast.5), channel_id=1, replica_groups={{0,1,2,3,4,5,6,7,8,9,10,11,12,13,14,15},{16,17,18,19,20,21,22,23,24,25,..., dimensions={0} | all-to-all | bytes 262144 | tf_op jit(solution)/shard_map/all_to_all | solution.py:308
  62.5 17.3 %all_to_all.21.parts_ref = bf16[16,16,256]{2,1,0:T(8,128)(2,1)S(1)} all-to-all(bf16[16,16,256]{2,1,0:T(8,128)(2,1)S(1)} %sum.2), channel_id=1, replica_groups={{0,16,32,48,64,80,96,112,128,144,160,176,192,208,224,240},{1,17,33,49,6..., dimensions={0} | all-to-all | bytes 262144 | tf_op jit(solution)/shard_map/all_to_all | solution.py:308
  79.8 0.7 sum.3
  80.5 4.7 %all-to-all-start.3 = ((bf16[16,16,256]{2,1,0:T(8,128)(2,1)}), bf16[16,16,256]{2,1,0:T(8,128)(2,1)S(1)}, u32[]{:S(2)}, u32[]{:S(2)}) async-start(bf16[16,16,256]{2,1,0:T(8,128)(2,1)} %sum.3), calls=%async_computation.3 | async-start | bytes 262144 | tf_op jit(solution)/shard_map/all_to_all | solution.py:308
  85.4 1.4 %collective-permute-start.7 = (bf16[16,16,128]{2,1,0:T(8,128)(2,1)S(1)}, bf16[16,16,128]{2,1,0:T(8,128)(2,1)S(1)}, u32[]{:S(2)}, u32[]{:S(2)}) collective-permute-start(bf16[16,16,128]{2,1,0:T(8,128)(2,1)S(1)} %get-tuple-element.38), channel_id=1, source_target_pairs={{0,2},{1,3},{2,0},{3,1},{4,6},{5,7},{6,4},{7,5},{8,10},{9,11},{10,... | collective-permute-start | bytes 196616 | tf_op jit(solution)/shard_map/ppermute | solution.py:355
  87.3 4.3 %collective-permute-done.7.got2_ref = bf16[16,16,128]{2,1,0:T(8,128)(2,1)S(1)} collective-permute-done((bf16[16,16,128]{2,1,0:T(8,128)(2,1)S(1)}, bf16[16,16,128]{2,1,0:T(8,128)(2,1)S(1)}, u32[]{:S(2)}, u32[]{:S(2)}) %collective-permute-start.7) | collective-permute-done | bytes 65568 | tf_op jit(solution)/shard_map/ppermute | solution.py:355
  91.6 2.0 %collective-permute-done.8.got3_ref = bf16[16,16,128]{2,1,0:T(8,128)(2,1)S(1)} collective-permute-done((bf16[16,16,128]{2,1,0:T(8,128)(2,1)S(1)}, bf16[16,16,128]{2,1,0:T(8,128)(2,1)S(1)}, u32[]{:S(2)}, u32[]{:S(2)}) %collective-permute-start.8) | collective-permute-done | bytes 65568 | tf_op jit(solution)/shard_map/ppermute | solution.py:355
  93.5 1.0 %all-to-all-done.3.grad_ref = bf16[16,16,256]{2,1,0:T(8,128)(2,1)S(1)} async-done(((bf16[16,16,256]{2,1,0:T(8,128)(2,1)}), bf16[16,16,256]{2,1,0:T(8,128)(2,1)S(1)}, u32[]{:S(2)}, u32[]{:S(2)}) %all-to-all-start.3) | async-done | bytes 131104 | tf_op jit(solution)/shard_map/all_to_all | solution.py:308
  94.5 1.0 %unpack.1 = (f32[3,3,3,16,16]{4,3,2,1,0:T(8,128)}, f32[3,3,3,16,64]{4,3,2,1,0:T(8,128)}, bf16[16,1,64,128]{3,2,1,0:T(8,128)(2,1)}) custom-call(bf16[16,16,256]{2,1,0:T(8,128)(2,1)S(1)} %all-to-all-done.3.grad_ref, bf16[16,16,128]{2,1,0:T(8,128)(2,1)S(1)} %get-tuple-element.36.got0_ref, bf16[16,16,128]{2,1,0:T(8,128)(2,1)S(1)} %collective-permute-done.6.got1_ref, ...), custom_call_target="tpu_custom_call" | custom-call | flops 2000000000 | bytes 1000000 | tf_op jit(solution)/shard_map/unpack/pallas_call | solution.py:363
  (17 shorter events, 1.3 us)
Async XLA Ops:
  0.6 16.6 %copy-start.3 = (bf16[64,16,3,3,3]{0,1,4,3,2:T(8,128)(2,1)S(1)}, bf16[64,16,3,3,3]{0,1,4,3,2:T(8,128)(2,1)}, u32[]{:S(2)}) copy-start(bf16[64,16,3,3,3]{0,1,4,3,2:T(8,128)(2,1)} %param.6) | copy-start | bytes 165892
  0.6 16.6 %copy-start.2 = (bf16[16,16,3,3,3]{1,0,4,3,2:T(8,128)(2,1)S(1)}, bf16[16,16,3,3,3]{1,0,4,3,2:T(8,128)(2,1)}, u32[]{:S(2)}) copy-start(bf16[16,16,3,3,3]{1,0,4,3,2:T(8,128)(2,1)} %param.5) | copy-start | bytes 41476
  3.1 14.6 %all-to-all-start = ((bf16[4,30,16,128]{3,2,1,0:T(8,128)(2,1)}), bf16[4,30,16,128]{3,2,1,0:T(8,128)(2,1)S(1)}, u32[]{:S(2)}, u32[]{:S(2)}) async-start(bf16[4,30,16,128]{3,2,1,0:T(8,128)(2,1)} %get-tuple-element.25), calls=%async_computation | async-start | bytes 983040 | tf_op jit(solution)/shard_map/all_to_all | solution.py:323
  9.8 18.8 %collective-permute-start = (bf16[32,16,256]{2,1,0:T(8,128)(2,1)}, bf16[32,16,256]{2,1,0:T(8,128)(2,1)S(1)}, u32[]{:S(2)}, u32[]{:S(2)}) collective-permute-start(bf16[32,16,256]{2,1,0:T(8,128)(2,1)} %get-tuple-element.23.b_ref), channel_id=1, source_target_pairs={{4,8},{8,4},{12,16},{16,12},{20,24},{24,20},{28,32},{32,28},{36,40... | collective-permute-start | bytes 786440 | tf_op jit(solution)/shard_map/ppermute | solution.py:304
  10.4 19.2 %collective-permute-start.1 = (bf16[32,16,256]{2,1,0:T(8,128)(2,1)}, bf16[32,16,256]{2,1,0:T(8,128)(2,1)S(1)}, u32[]{:S(2)}, u32[]{:S(2)}) collective-permute-start(bf16[32,16,256]{2,1,0:T(8,128)(2,1)} %get-tuple-element.24.c_ref), channel_id=1, source_target_pairs={{0,4},{4,0},{8,12},{12,8},{16,20},{20,16},{24,28},{28,24},{32,36},... | collective-permute-start | bytes 786440 | tf_op jit(solution)/shard_map/ppermute | solution.py:304
  17.8 15.8 %copy-start = (bf16[32,16,256]{2,1,0:T(8,128)(2,1)S(1)}, bf16[32,16,256]{2,1,0:T(8,128)(2,1)}, u32[]{:S(2)}) copy-start(bf16[32,16,256]{2,1,0:T(8,128)(2,1)} %get-tuple-element.24.c_ref) | copy-start | bytes 786436
  17.8 15.7 %copy-start.1 = (bf16[32,16,256]{2,1,0:T(8,128)(2,1)S(1)}, bf16[32,16,256]{2,1,0:T(8,128)(2,1)}, u32[]{:S(2)}) copy-start(bf16[32,16,256]{2,1,0:T(8,128)(2,1)} %get-tuple-element.23.b_ref) | copy-start | bytes 786436
  18.4 11.3 %collective-permute-start.2 = (bf16[28,16,128]{2,1,0:T(8,128)(2,1)S(1)}, bf16[28,16,128]{2,1,0:T(8,128)(2,1)S(1)}, u32[]{:S(2)}, u32[]{:S(2)}) collective-permute-start(bf16[28,16,128]{2,1,0:T(8,128)(2,1)S(1)} %get-tuple-element.27.mb_ref), channel_id=1, source_target_pairs={{4,8},{8,4},{12,16},{16,12},{20,24},{24,20},{28,32},{32,28},{36,40... | collective-permute-start | bytes 344072 | tf_op jit(solution)/shard_map/ppermute | solution.py:304
  19.0 14.5 %collective-permute-start.3 = (bf16[28,16,128]{2,1,0:T(8,128)(2,1)S(1)}, bf16[28,16,128]{2,1,0:T(8,128)(2,1)S(1)}, u32[]{:S(2)}, u32[]{:S(2)}) collective-permute-start(bf16[28,16,128]{2,1,0:T(8,128)(2,1)S(1)} %get-tuple-element.28.mc_ref), channel_id=1, source_target_pairs={{0,4},{4,0},{8,12},{12,8},{16,20},{20,16},{24,28},{28,24},{32,36},... | collective-permute-start | bytes 344072 | tf_op jit(solution)/shard_map/ppermute | solution.py:304
  34.8 4.9 %collective-permute-start.5 = (bf16[18,16,128]{2,1,0:T(8,128)(2,1)S(1)}, bf16[18,16,128]{2,1,0:T(8,128)(2,1)S(1)}, u32[]{:S(2)}, u32[]{:S(2)}) collective-permute-start(bf16[18,16,128]{2,1,0:T(8,128)(2,1)S(1)} %get-tuple-element.30.own_ref), channel_id=1, source_target_pairs={{4,8},{8,4},{12,16},{16,12},{20,24},{24,20},{28,32},{32,28},{36,40... | collective-permute-start | bytes 221192 | tf_op jit(solution)/shard_map/ppermute | solution.py:304
  35.5 4.9 %collective-permute-start.4 = (bf16[18,16,128]{2,1,0:T(8,128)(2,1)S(1)}, bf16[18,16,128]{2,1,0:T(8,128)(2,1)S(1)}, u32[]{:S(2)}, u32[]{:S(2)}) collective-permute-start(bf16[18,16,128]{2,1,0:T(8,128)(2,1)S(1)} %get-tuple-element.30.own_ref), channel_id=1, source_target_pairs={{0,4},{4,0},{8,12},{12,8},{16,20},{20,16},{24,28},{28,24},{32,36},... | collective-permute-start | bytes 221192 | tf_op jit(solution)/shard_map/ppermute | solution.py:304
  80.5 14.1 %all-to-all-start.3 = ((bf16[16,16,256]{2,1,0:T(8,128)(2,1)}), bf16[16,16,256]{2,1,0:T(8,128)(2,1)S(1)}, u32[]{:S(2)}, u32[]{:S(2)}) async-start(bf16[16,16,256]{2,1,0:T(8,128)(2,1)} %sum.3), calls=%async_computation.3 | async-start | bytes 262144 | tf_op jit(solution)/shard_map/all_to_all | solution.py:308
  85.1 2.1 %collective-permute-start.6 = (bf16[16,16,128]{2,1,0:T(8,128)(2,1)S(1)}, bf16[16,16,128]{2,1,0:T(8,128)(2,1)S(1)}, u32[]{:S(2)}, u32[]{:S(2)}) collective-permute-start(bf16[16,16,128]{2,1,0:T(8,128)(2,1)S(1)} %get-tuple-element.37), channel_id=1, source_target_pairs={{0,1},{1,0},{2,3},{3,2},{4,5},{5,4},{6,7},{7,6},{8,9},{9,8},{10,11... | collective-permute-start | bytes 196616 | tf_op jit(solution)/shard_map/ppermute | solution.py:355
  85.4 6.1 %collective-permute-start.7 = (bf16[16,16,128]{2,1,0:T(8,128)(2,1)S(1)}, bf16[16,16,128]{2,1,0:T(8,128)(2,1)S(1)}, u32[]{:S(2)}, u32[]{:S(2)}) collective-permute-start(bf16[16,16,128]{2,1,0:T(8,128)(2,1)S(1)} %get-tuple-element.38), channel_id=1, source_target_pairs={{0,2},{1,3},{2,0},{3,1},{4,6},{5,7},{6,4},{7,5},{8,10},{9,11},{10,... | collective-permute-start | bytes 196616 | tf_op jit(solution)/shard_map/ppermute | solution.py:355
  86.9 6.7 %collective-permute-start.8 = (bf16[16,16,128]{2,1,0:T(8,128)(2,1)S(1)}, bf16[16,16,128]{2,1,0:T(8,128)(2,1)S(1)}, u32[]{:S(2)}, u32[]{:S(2)}) collective-permute-start(bf16[16,16,128]{2,1,0:T(8,128)(2,1)S(1)} %get-tuple-element.39), channel_id=1, source_target_pairs={{0,3},{1,2},{2,1},{3,0},{4,7},{5,6},{6,5},{7,4},{8,11},{9,10},{10,... | collective-permute-start | bytes 196616 | tf_op jit(solution)/shard_map/ppermute | solution.py:355

commit v2 on v1

--- a/solution.py
+++ b/solution.py
@@ -1,5 +1,3 @@
-import functools
-
 import jax
 import jax.numpy as jnp
 from jax import lax
@@ -47,8 +45,8 @@
     return jnp.where(iota(x.shape, 1) == edge, 0.0, pltpu.roll(x, step % width, 1))
 
 
-def call(body, outs, scratch=(), flops=2_000_000_000, n_in=1, spec=VMEM, vmem=32 * 1024 * 1024, name=None):
-    specs = [spec] * n_in
+def call(body, outs, scratch=(), flops=2_000_000_000, n_in=1, spec=VMEM, unread=0, vmem=32 * 1024 * 1024):
+    specs = [spec] * n_in + [pl.BlockSpec(memory_space=pl.ANY)] * unread
     return pl.pallas_call(
         body,
         out_shape=tuple(jax.ShapeDtypeStruct(s, d) for s, d in outs),
@@ -57,27 +55,27 @@
         scratch_shapes=scratch,
         cost_estimate=pl.CostEstimate(flops=flops, bytes_accessed=1_000_000, transcendentals=0),
         compiler_params=pltpu.CompilerParams(vmem_limit_bytes=vmem),
-        name=name,
     )
 
 
-def pack_kernel(vol_hbm, cot_hbm, near_ref, far_ref, pay_ref, vol_ref, cot_ref, sems):
+def pack_kernel(vol_hbm, near_ref, far_ref, edge1_ref, edge3_ref, vol_ref, sem):
     fil, odd = position()
-    loads = [
-        pltpu.make_async_copy(vol_hbm, vol_ref, sems.at[0]),
-        pltpu.make_async_copy(cot_hbm, cot_ref, sems.at[1]),
-    ]
-    for load in loads:
-        load.start()
+    load = pltpu.make_async_copy(vol_hbm, vol_ref, sem.at[0])
+    load.start()
     swap = swap_matrix()
-    planes = (near_ref, far_ref)
-    loads[0].wait()
-    for which, v_ref in enumerate(planes):
+    load.wait()
+    for which, v_ref in enumerate((near_ref, far_ref)):
         x = 1 - odd if which == 0 else odd
         for half in range(2):
             block = vol_ref[:, pl.ds(x, 1), 16 * half : 16 * half + 16, :].reshape(256, 256)
             v_ref[16 * half : 16 * half + 16] = dot(swap, block).astype(BF16).reshape(16, 16, 256)
-    loads[1].wait()
+        low, high = v_ref[0:3], v_ref[29:32]
+        edge1_ref[3 * which : 3 * which + 3] = jnp.where(lax.rem(fil, 2) == 0, high, low)
+        edge3_ref[3 * which : 3 * which + 3] = jnp.where(fil < 2, high, low)
+
+
+def pack_cot_kernel(cot_ref, after_ref, pay_ref):
+    swap = swap_matrix()
     for dest in range(4):
         block = cot_ref[:, 0, 16 * dest : 16 * dest + 16, :].reshape(256, 128)
         rows = dot(swap, block).astype(BF16).reshape(16, 16, 128)
@@ -90,24 +88,32 @@
             pay_ref[dest - 1, 17] = rows[0]
         else:
             pay_ref[3, 17] = jnp.zeros((16, 128), BF16)
-    for dest in range(4):
-        for which, v_ref in enumerate(planes):
-            for side in range(2):
-                at = 18 + 6 * side + 3 * which
-                lanes = slice(128 * side, 128 * side + 128)
-                rows = jnp.where(dest > fil, v_ref[29:32, :, lanes], v_ref[0:3, :, lanes])
-                pay_ref[dest, at : at + 3] = rows
-
-
-def weights_kernel(fk_ref, ck_ref, w1_ref, w2_ref, w4_ref):
+
+
+def extend_kernel(near_ref, far_ref, edge1_ref, edge3_ref, near_out, far_out):
+    fil, _ = position()
+    upper = lax.rem(fil, 2) == 1
+    for which, (v_ref, out_ref) in enumerate(((near_ref, near_out), (far_ref, far_out))):
+        rows = slice(3 * which, 3 * which + 3)
+        out_ref[3:35] = v_ref[...]
+        out_ref[0:3] = jnp.where(upper, edge1_ref[rows], edge3_ref[rows])
+        out_ref[35:38] = jnp.where(upper, edge3_ref[rows], edge1_ref[rows])
+
+
+def returned_weights(ck_ref):
     row, col = iota((64, 256), 0), iota((64, 256), 1)
+    slots = []
     for slot in range(2):
         total = None
         for dy in range(3):
             place = jnp.where(col == (row // 16) * 64 + (slot + 2 - dy) * 16 + row % 16, 1.0, 0.0).astype(BF16)
             part = dot(ck_ref[:, dy].reshape(144, 64), place)
             total = part if total is None else total + part
-        w1_ref[144 * slot : 144 * slot + 144] = total.astype(BF16)
+        slots.append(total.astype(BF16))
+    return jnp.concatenate(slots, 0)
+
+
+def fine_weights_kernel(fk_ref, w2_ref):
     row, col = iota((16, 256), 0), iota((16, 256), 1)
     total = None
     for dx in range(3):
@@ -122,6 +128,9 @@
             for dz in range(3):
                 at = 64 * dz + 32 * x + 16 * y
                 w2_ref[at : at + 16] = rolled[16 * dz : 16 * dz + 16]
+
+
+def coarse_weights_kernel(ck_ref, after_ref, w4_ref):
     eye = jnp.where(iota((64, 64), 0) == iota((64, 64), 1), 1.0, 0.0).astype(BF16)
     zero = jnp.zeros((16, 64), BF16)
     for dz in range(3):
@@ -135,25 +144,11 @@
             w4_ref[at : at + 64] = dot_t(eye, jnp.concatenate(rows, 0)).astype(BF16)
 
 
-def returned_kernel(got_ref, w1_ref, own_ref, near_ref, far_ref):
-    fil, odd = position()
-    before = jnp.maximum(fil - 1, 0)
-    after = jnp.minimum(fil + 1, 3)
-    for which, msg_ref in enumerate((near_ref, far_ref)):
-        for side in range(2):
-            at = 18 + 6 * side + 3 * which
-            msg_ref[16 + 3 * side : 19 + 3 * side] = got_ref[before, at : at + 3]
-            msg_ref[22 + 3 * side : 25 + 3 * side] = got_ref[after, at : at + 3]
-
-        @pl.when(fil == 0)
-        def _():
-            msg_ref[16:22] = jnp.zeros((6, 16, 128), BF16)
-
-        @pl.when(fil == 3)
-        def _():
-            msg_ref[22:28] = jnp.zeros((6, 16, 128), BF16)
-
-    w1 = w1_ref[...]
+def returned_kernel(got_ref, ck_ref, pooled_ref, own_ref, near_ref, far_ref):
+    _, odd = position()
+    near_ref[0:18] = pooled_ref[...]
+    far_ref[0:18] = pooled_ref[...]
+    w1 = returned_weights(ck_ref)
     for pair in range(8):
         window = got_ref[:, 2 * pair : 2 * pair + 4].reshape(256, 128)
         product = dot(w1, window).reshape(2, 3, 3, 16, 128)
@@ -162,8 +157,8 @@
                 moved(product[slot, tx, 0], -1) + product[slot, tx, 1] + moved(product[slot, tx, 2], 1) for tx in range(3)
             ]
             own_ref[2 * pair + slot] = own
-            near_ref[2 * pair + slot] = jnp.where(odd == 0, high, low).astype(BF16)
-            far_ref[2 * pair + slot] = jnp.where(odd == 0, low, high).astype(BF16)
+            near_ref[18 + 2 * pair + slot] = jnp.where(odd == 0, high, low).astype(BF16)
+            far_ref[18 + 2 * pair + slot] = jnp.where(odd == 0, low, high).astype(BF16)
 
 
 def window_of(refs, start, count):
@@ -174,16 +169,10 @@
     return [ref.at[x] for x in range(4)]
 
 
-def fine_kernel_body(a_ref, b_ref, c_ref, d_ref, ma_ref, mb_ref, mc_ref, md_ref, w2_ref, pooled_ref, mask_ref, all_ref, sums):
+def fine_kernel_body(a_ref, b_ref, c_ref, d_ref, w2_ref, pooled_ref, mask_ref, all_ref, sums):
     fil, odd = position()
-    messages = (ma_ref, mb_ref, mc_ref, md_ref)
     for k, v_ref in enumerate((a_ref, b_ref, c_ref, d_ref)):
-        x = k + odd * (3 - 2 * k)
-        all_ref[x, 3:35] = v_ref[...]
-        for side in range(2):
-            lanes = slice(128 * side, 128 * side + 128)
-            all_ref[x, 0:3, :, lanes] = messages[k][16 + 3 * side : 19 + 3 * side]
-            all_ref[x, 35:38, :, lanes] = messages[k][22 + 3 * side : 25 + 3 * side]
+        all_ref[k + odd * (3 - 2 * k)] = v_ref[...]
 
     def block(b):
         window = window_of(planes_of(all_ref), 2 * b, 4)
@@ -217,8 +206,8 @@
     pooled_ref[...] = (dot(high, pool) + dot(low, pool)).astype(BF16).reshape(18, 16, 128)
 
 
-def fine_grad_kernel(own_ref, low_ref, high_ref, all_ref, mask_ref, out_ref, up, acc):
-    total = own_ref[...] + (low_ref[0:16].astype(F32) + high_ref[0:16].astype(F32))
+def fine_grad_part(own_ref, near_msg, far_msg, all_ref, mask_ref, out_ref, up, acc):
+    total = own_ref[...] + (near_msg[18:34].astype(F32) + far_msg[18:34].astype(F32))
     scaled = (total * 0.125).astype(BF16).reshape(256, 128)
     spread = jnp.where(iota((128, 256), 0) == iota((128, 256), 1) // 2, 1.0, 0.0).astype(BF16)
     up[...] = dot(scaled, spread).reshape(16, 16, 256)
@@ -241,11 +230,15 @@
         out_ref[16 * t : 16 * t + 16] = total
 
 
-def coarse_kernel_body(near_ref, own_ref, far_ref, got_ref, w4_ref, fine_ref, out0_ref, out1_ref, out2_ref, out3_ref, grad_ref, rows_out, acc, slab):
+def last_kernel(
+    own_r, near_msg, own_msg, far_msg, got_ref, all_ref, mask_ref, w4_ref,
+    out0_ref, out1_ref, out2_ref, out3_ref, grad_ref, rows_out, acc, slab, up, fine_acc, fine_ref,
+):
     fil, odd = position()
-    slab[2 - 2 * odd] = near_ref[...]
-    slab[1] = own_ref[...]
-    slab[2 * odd] = far_ref[...]
+    fine_grad_part(own_r, near_msg, far_msg, all_ref, mask_ref, fine_ref, up, fine_acc)
+    slab[2 - 2 * odd] = near_msg[0:18]
+    slab[1] = own_msg[0:18]
+    slab[2 * odd] = far_msg[0:18]
     acc[...] = jnp.zeros_like(acc)
     pad = jnp.zeros((64, 128), BF16)
 
@@ -301,7 +294,9 @@
     count = lax.axis_size("vox")
     first = [(i, i ^ 1) for i in range(count)]
     second = [(i, ((i + 1) ^ 1) - 1) for i in range(1, count - 1)]
-    return lax.ppermute(near, "vox", first), lax.ppermute(far, "vox", second)
+    near = lax.ppermute(near, "vox", first)
+    far = lax.ppermute(far, "vox", second)
+    return near, far
 
 
 def exchange(pieces, groups):
@@ -309,62 +304,58 @@
 
 
 def local(volume, fine_kernel, coarse_kernel, coarse_cot):
-    plane = ((32, 16, 256), BF16)
-    near, far, pay = call(
+    plane, edge, wide = ((32, 16, 256), BF16), ((6, 16, 256), BF16), ((38, 16, 256), BF16)
+    near, far, edge1, edge3 = call(
         pack_kernel,
-        [plane, plane, ((4, 30, 16, 128), BF16)],
-        scratch=[pltpu.VMEM(volume.shape, BF16), pltpu.VMEM(coarse_cot.shape, BF16), pltpu.SemaphoreType.DMA((2,))],
-        n_in=2,
+        [plane, plane, edge, edge],
+        scratch=[pltpu.VMEM(volume.shape, BF16), pltpu.SemaphoreType.DMA((1,))],
+        n_in=1,
         spec=HBM,
-        vmem=63 * 1024 * 1024,
-        name="pack",
-    )(volume, coarse_cot)
+    )(volume)
+    (pay,) = call(pack_cot_kernel, [((4, 18, 16, 128), BF16)], n_in=1, unread=1)(coarse_cot, edge1)
+    edge1 = lax.ppermute(edge1, "fil", [(i, i ^ 1) for i in range(4)])
+    edge3 = lax.ppermute(edge3, "fil", [(1, 2), (2, 1)])
+    got = lax.all_to_all(pay, "fil", 0, 0, tiled=True)
+    near, far = call(extend_kernel, [wide, wide], n_in=4)(near, far, edge1, edge3)
     near_got, far_got = swapped(near, far)
-    got = lax.all_to_all(pay, "fil", 0, 0, tiled=True)
-    w1, w2, w4 = call(
-        weights_kernel, [((288, 256), BF16), ((192, 256), BF16), ((384, 256), BF16)], n_in=2, name="weights"
-    )(fine_kernel.transpose(2, 3, 4, 0, 1), coarse_kernel.transpose(2, 3, 4, 1, 0))
-    message = ((28, 16, 128), BF16)
-    own, near_msg, far_msg = call(
-        returned_kernel, [((16, 16, 128), F32), message, message], n_in=2, name="returned"
-    )(got, w1)
-    near_msg_got, far_msg_got = swapped(near_msg, far_msg)
+    (w2,) = call(fine_weights_kernel, [((192, 256), BF16)], n_in=1)(fine_kernel.transpose(2, 3, 4, 0, 1))
+    coarse_taps = coarse_kernel.transpose(2, 3, 4, 1, 0)
     pooled, mask, cells = call(
         fine_kernel_body,
         [((18, 16, 128), BF16), ((16, 64, 256), BF16), ((4, 38, 16, 256), BF16)],
         scratch=[pltpu.VMEM((18, 16, 256), F32)],
-        n_in=9,
-        name="fine",
-    )(far_got, far, near, near_got, far_msg_got, far_msg, near_msg, near_msg_got, w2)
-    pooled_near, pooled_far = swapped(pooled, pooled)
-    (fine_part,) = call(
-        fine_grad_kernel,
-        [((48, 256), F32)],
-        scratch=[pltpu.VMEM((16, 16, 256), F32), pltpu.VMEM((192, 256), F32)],
         n_in=5,
-        name="fine_grad",
-    )(own, near_msg_got, far_msg_got, cells, mask)
+    )(far_got, far, near, near_got, w2)
+    message = ((34, 16, 128), BF16)
+    own_r, near_msg, far_msg = call(
+        returned_kernel, [((16, 16, 128), F32), message, message], n_in=3
+    )(got, coarse_taps, pooled)
+    (w4,) = call(coarse_weights_kernel, [((384, 256), BF16)], n_in=1, unread=1)(coarse_taps, near_msg)
+    near_msg_got, far_msg_got = swapped(near_msg, far_msg)
     *out_pieces, grads = call(
-        coarse_kernel_body,
+        last_kernel,
         [((16, 16, 128), BF16)] * 4 + [((256, 256), BF16)],
-        scratch=[pltpu.VMEM((4, 16, 16, 128), BF16), pltpu.VMEM((384, 256), F32), pltpu.VMEM((3, 18, 16, 128), BF16)],
-        n_in=6,
-        name="coarse",
-    )(pooled_near, pooled, pooled_far, got, w4, fine_part)
+        scratch=[
+            pltpu.VMEM((4, 16, 16, 128), BF16),
+            pltpu.VMEM((384, 256), F32),
+            pltpu.VMEM((3, 18, 16, 128), BF16),
+            pltpu.VMEM((16, 16, 256), F32),
+            pltpu.VMEM((192, 256), F32),
+            pltpu.VMEM((48, 256), F32),
+        ],
+        n_in=8,
+    )(own_r, near_msg_got, near_msg, far_msg_got, got, cells, mask, w4)
     out_got = out_pieces[:1] + [
         lax.ppermute(out_pieces[k], "fil", [(i, i ^ k) for i in range(4)]) for k in range(1, 4)
     ]
     lines = [[16 * g + j for j in range(16)] for g in range(16)]
     sheets = [[16 * g + j for g in range(16)] for j in range(16)]
-    summed = call(sum_kernel, [((16, 16, 256), BF16)], name="sum")
+    summed = call(sum_kernel, [((16, 16, 256), BF16)])
     parts = exchange(grads.reshape(16, 16, 256), lines)
     parts = exchange(summed(parts)[0], sheets)
     spread = exchange(summed(parts)[0], lines)
     grad_fine, grad_coarse, coarse_out = call(
-        unpack_kernel,
-        [((3, 3, 3, 16, 16), F32), ((3, 3, 3, 16, 64), F32), ((16, 1, 64, 128), BF16)],
-        n_in=5,
-        name="unpack",
+        unpack_kernel, [((3, 3, 3, 16, 16), F32), ((3, 3, 3, 16, 64), F32), ((16, 1, 64, 128), BF16)], n_in=5
     )(spread, *out_got)
     return (coarse_out, grad_fine.transpose(3, 4, 0, 1, 2), grad_coarse.transpose(4, 3, 0, 1, 2))
 

time: 95.9 us -> 94 us (0.980)
  waiting for transfers between devices: 12.9 us -> 22.1 us
  starting transfers between devices: 34.9 us -> 26.2 us
  blocking collectives: 38 us -> 35.5 us
  Pallas kernels: 8.98 us -> 7.88 us
  local copies, waits for them, and re-layouts: 0.02 us -> 1.05 us
    ppermute x6, waiting for transfers between devices: 5.67 us -> 14 us  [the longest x2 10.5 us: swapped(): near = lax.ppermute(near, 'vox', first)]
    ppermute x6, starting transfers between devices: 21.5 us -> 16 us  [the longest x2 9.33 us: swapped(): near = lax.ppermute(near, 'vox', first)]
    all_to_all x1, starting transfers between devices: 6.65 us -> 3.44 us  [local(): got = lax.all_to_all(pay, 'fil', 0, 0, tiled=True)]
    all_to_all x2, blocking collectives: 38 us -> 35.5 us  [exchange(): lax.all_to_all(pieces, ('vox', 'fil'), 0, 0, tiled=True, axis_index_group...]
    pallas_call x5 -> x7, Pallas kernels: 5.93 us -> 4.86 us  [the longest x1 2.1 us: local(): call(last_kernel, [((16, 16, 128), BF16)] * 4 + [((256, 256), BF16)], scr...]
    unnamed x8, local copies, waits for them, and re-layouts: 0.02 us -> 1.05 us
  transfers between devices with their start and end apart: 11 -> 11, of which waited for: 6 -> 7; matrix products, arithmetic and copies ran while one was open for 0% -> 0% of each run, Pallas kernels for 2% -> 3%
where the time goes in v2:
time: 94 us; the launch traced here: 93.6 us
  blocking collectives  35.5 us (38%)
  starting transfers between devices  26.2 us (28%)
  waiting for transfers between devices  22.1 us (24%)
  Pallas kernels  7.88 us (8%)
  local copies, waits for them, and re-layouts  1.05 us (1%)
    all_to_all x2, blocking collectives, exchange(): lax.all_to_all(pieces, ('vox', 'fil'), 0, 0, tiled=True, axis_index_group...  35.5 us
    ppermute x2, waiting for transfers between devices, swapped(): near = lax.ppermute(near, 'vox', first)  10.5 us
    ppermute x2, starting transfers between devices, swapped(): near = lax.ppermute(near, 'vox', first)  9.33 us
    ppermute x3, waiting for transfers between devices, local(): lax.ppermute(out_pieces[k], 'fil', [(i, i ^ k) for i in range(4)])  6.29 us
    all_to_all x1, starting transfers between devices, exchange(): lax.all_to_all(pieces, ('vox', 'fil'), 0, 0, tiled=True, axis_index_group...  4.65 us
    ppermute x1, waiting for transfers between devices, local(): edge3 = lax.ppermute(edge3, 'fil', [(1, 2), (2, 1)])  3.47 us
    all_to_all x1, starting transfers between devices, local(): got = lax.all_to_all(pay, 'fil', 0, 0, tiled=True)  3.44 us
    ppermute x1, starting transfers between devices, local(): edge1 = lax.ppermute(edge1, 'fil', [(i, i ^ 1) for i in range(4)])  3.29 us
  transfers between devices with their start and end apart: 11, of which 7 were waited for; matrix products, arithmetic and copies ran while one was open for 0% of the time, Pallas kernels for 3%

profile of v2, /device:TPU:1, one launch (start us, length us, event | category | flops | bytes accessed | tf_op | source)
XLA Modules:
  0.0 93.6 jit_solution(3462494701028406621)
XLA Ops:
  0.6 1.0 %copy-done = bf16[16,2,32,256]{3,2,1,0:T(8,128)(2,1)S(1)} copy-done((bf16[16,2,32,256]{3,2,1,0:T(8,128)(2,1)S(1)}, bf16[16,2,32,256]{3,2,1,0:T(8,128)(2,1)}, u32[]{:S(2)}) %copy-start) | copy-done | bytes 524312
  2.1 3.3 %collective-permute-start = (bf16[6,16,256]{2,1,0:T(8,128)(2,1)S(1)}, bf16[6,16,256]{2,1,0:T(8,128)(2,1)S(1)}, u32[]{:S(2)}, u32[]{:S(2)}) collective-permute-start(bf16[6,16,256]{2,1,0:T(8,128)(2,1)S(1)} %get-tuple-element.23.after_ref), channel_id=1, source_target_pairs={{0,1},{1,0},{2,3},{3,2},{4,5},{5,4},{6,7},{7,6},{8,9},{9,8},{10,11... | collective-permute-start | bytes 147464 | tf_op jit(solution)/shard_map/ppermute | solution.py:316
  5.4 1.9 %collective-permute-start.1 = (bf16[6,16,256]{2,1,0:T(8,128)(2,1)S(1)}, bf16[6,16,256]{2,1,0:T(8,128)(2,1)S(1)}, u32[]{:S(2)}, u32[]{:S(2)}) collective-permute-start(bf16[6,16,256]{2,1,0:T(8,128)(2,1)S(1)} %get-tuple-element.26), channel_id=1, source_target_pairs={{1,2},{2,1},{5,6},{6,5},{9,10},{10,9},{13,14},{14,13},{17,18},{18,... | collective-permute-start | bytes 147464 | tf_op jit(solution)/shard_map/ppermute | solution.py:317
  7.3 3.5 %collective-permute-done.1.edge3_ref = bf16[6,16,256]{2,1,0:T(8,128)(2,1)S(1)} collective-permute-done((bf16[6,16,256]{2,1,0:T(8,128)(2,1)S(1)}, bf16[6,16,256]{2,1,0:T(8,128)(2,1)S(1)}, u32[]{:S(2)}, u32[]{:S(2)}) %collective-permute-start.1) | collective-permute-done | bytes 49184 | tf_op jit(solution)/shard_map/ppermute | solution.py:317
  10.8 0.8 collective-permute-start.2
  11.6 7.3 %collective-permute-start.3 = (bf16[38,16,256]{2,1,0:T(8,128)(2,1)S(1)}, bf16[38,16,256]{2,1,0:T(8,128)(2,1)S(1)}, u32[]{:S(2)}, u32[]{:S(2)}) collective-permute-start(bf16[38,16,256]{2,1,0:T(8,128)(2,1)S(1)} %get-tuple-element.28.c_ref), channel_id=1, source_target_pairs={{0,4},{4,0},{8,12},{12,8},{16,20},{20,16},{24,28},{28,24},{32,36},... | collective-permute-start | bytes 933896 | tf_op jit(solution)/shard_map/ppermute | solution.py:297
  18.9 1.0 %shard_map.68 = bf16[4,18,16,128]{3,2,1,0:T(8,128)(2,1)} custom-call(bf16[16,1,64,128]{3,2,1,0:T(8,128)(2,1)S(1)} %copy-done.1, bf16[6,16,256]{2,1,0:T(8,128)(2,1)S(1)} %get-tuple-element.23.after_ref), custom_call_target="tpu_custom_call" | custom-call | flops 2000000000 | bytes 1000000 | tf_op jit(solution)/shard_map/pallas_call | solution.py:315
  19.9 3.4 %all-to-all-start = ((bf16[4,18,16,128]{3,2,1,0:T(8,128)(2,1)}), bf16[4,18,16,128]{3,2,1,0:T(8,128)(2,1)S(1)}, u32[]{:S(2)}, u32[]{:S(2)}) async-start(bf16[4,18,16,128]{3,2,1,0:T(8,128)(2,1)} %shard_map.68), calls=%async_computation | async-start | bytes 589824 | tf_op jit(solution)/shard_map/all_to_all | solution.py:318
  23.7 5.0 %collective-permute-done.3.d_ref = bf16[38,16,256]{2,1,0:T(8,128)(2,1)S(1)} collective-permute-done((bf16[38,16,256]{2,1,0:T(8,128)(2,1)S(1)}, bf16[38,16,256]{2,1,0:T(8,128)(2,1)S(1)}, u32[]{:S(2)}, u32[]{:S(2)}) %collective-permute-start.3) | collective-permute-done | bytes 311328 | tf_op jit(solution)/shard_map/ppermute | solution.py:297
  28.7 1.3 %shard_map.71 = (bf16[18,16,128]{2,1,0:T(8,128)(2,1)S(1)}, bf16[16,64,256]{2,1,0:T(8,128)(2,1)S(1)}, bf16[4,38,16,256]{3,2,1,0:T(8,128)(2,1)S(1)}) custom-call(bf16[38,16,256]{2,1,0:T(8,128)(2,1)S(1)} %collective-permute-done.2.a_ref, bf16[38,16,256]{2,1,0:T(8,128)(2,1)S(1)} %get-tuple-element.27.b_ref, bf16[38,16,256]{2,1,0:T(8,128)(2,1)S(1)} %get-tuple-element.28.c_ref, ...), custom_call_target="tpu_custom_call" | custom-call | flops 2000000000 | bytes 1000000 | tf_op jit(solution)/shard_map/pallas_call | solution.py:323
  30.0 0.9 all-to-all-done.got_ref
  30.9 0.7 shard_map.72
  31.6 2.0 %collective-permute-start.4 = (bf16[34,16,128]{2,1,0:T(8,128)(2,1)S(1)}, bf16[34,16,128]{2,1,0:T(8,128)(2,1)S(1)}, u32[]{:S(2)}, u32[]{:S(2)}) collective-permute-start(bf16[34,16,128]{2,1,0:T(8,128)(2,1)S(1)} %get-tuple-element.31.after_ref.own_msg), channel_id=1, source_target_pairs={{0,4},{4,0},{8,12},{12,8},{16,20},{20,16},{24,28},{28,24},{32,36},... | collective-permute-start | bytes 417800 | tf_op jit(solution)/shard_map/ppermute | solution.py:297
  34.6 5.5 %collective-permute-done.4.near_msg = bf16[34,16,128]{2,1,0:T(8,128)(2,1)S(1)} collective-permute-done((bf16[34,16,128]{2,1,0:T(8,128)(2,1)S(1)}, bf16[34,16,128]{2,1,0:T(8,128)(2,1)S(1)}, u32[]{:S(2)}, u32[]{:S(2)}) %collective-permute-start.4) | collective-permute-done | bytes 139296 | tf_op jit(solution)/shard_map/ppermute | solution.py:297
  40.1 2.1 %shard_map.74 = (bf16[16,16,128]{2,1,0:T(8,128)(2,1)S(1)}, bf16[16,16,128]{2,1,0:T(8,128)(2,1)S(1)}, bf16[16,16,128]{2,1,0:T(8,128)(2,1)S(1)}, bf16[16,16,128]{2,1,0:T(8,128)(2,1)S(1)}, bf16[256,256]{1,0:T(8,128)(2,1)S(1)}) custom-call(f32[16,16,128]{2,1,0:T(8,128)S(1)} %get-tuple-element.30.own_r, bf16[34,16,128]{2,1,0:T(8,128)(2,1)S(1)} %collective-permute-done.4.near_msg, ...), custom_call_target="tpu_custom_call" | custom-call | flops 2000000000 | bytes 1000000 | tf_op jit(solution)/shard_map/pallas_call | solution.py:335
  42.2 19.8 %all_to_all.20.parts_ref = bf16[16,16,256]{2,1,0:T(8,128)(2,1)S(1)} all-to-all(bf16[16,16,256]{2,1,0:T(8,128)(2,1)S(1)} %bitcast.5), channel_id=1, replica_groups={{0,1,2,3,4,5,6,7,8,9,10,11,12,13,14,15},{16,17,18,19,20,21,22,23,24,25,..., dimensions={0} | all-to-all | bytes 262144 | tf_op jit(solution)/shard_map/all_to_all | solution.py:303
  62.1 15.7 %all_to_all.21.parts_ref = bf16[16,16,256]{2,1,0:T(8,128)(2,1)S(1)} all-to-all(bf16[16,16,256]{2,1,0:T(8,128)(2,1)S(1)} %shard_map.75), channel_id=1, replica_groups={{0,16,32,48,64,80,96,112,128,144,160,176,192,208,224,240},{1,17,33,49,6..., dimensions={0} | all-to-all | bytes 262144 | tf_op jit(solution)/shard_map/all_to_all | solution.py:303
  77.8 0.7 shard_map.76
  78.5 4.7 %all-to-all-start.3 = ((bf16[16,16,256]{2,1,0:T(8,128)(2,1)}), bf16[16,16,256]{2,1,0:T(8,128)(2,1)S(1)}, u32[]{:S(2)}, u32[]{:S(2)}) async-start(bf16[16,16,256]{2,1,0:T(8,128)(2,1)} %shard_map.76), calls=%async_computation.3 | async-start | bytes 262144 | tf_op jit(solution)/shard_map/all_to_all | solution.py:303
  83.4 1.4 %collective-permute-start.7 = (bf16[16,16,128]{2,1,0:T(8,128)(2,1)S(1)}, bf16[16,16,128]{2,1,0:T(8,128)(2,1)S(1)}, u32[]{:S(2)}, u32[]{:S(2)}) collective-permute-start(bf16[16,16,128]{2,1,0:T(8,128)(2,1)S(1)} %get-tuple-element.38), channel_id=1, source_target_pairs={{0,2},{1,3},{2,0},{3,1},{4,6},{5,7},{6,4},{7,5},{8,10},{9,11},{10,... | collective-permute-start | bytes 196616 | tf_op jit(solution)/shard_map/ppermute | solution.py:349
  85.3 4.3 %collective-permute-done.7.got2_ref = bf16[16,16,128]{2,1,0:T(8,128)(2,1)S(1)} collective-permute-done((bf16[16,16,128]{2,1,0:T(8,128)(2,1)S(1)}, bf16[16,16,128]{2,1,0:T(8,128)(2,1)S(1)}, u32[]{:S(2)}, u32[]{:S(2)}) %collective-permute-start.7) | collective-permute-done | bytes 65568 | tf_op jit(solution)/shard_map/ppermute | solution.py:349
  89.6 2.0 %collective-permute-done.8.got3_ref = bf16[16,16,128]{2,1,0:T(8,128)(2,1)S(1)} collective-permute-done((bf16[16,16,128]{2,1,0:T(8,128)(2,1)S(1)}, bf16[16,16,128]{2,1,0:T(8,128)(2,1)S(1)}, u32[]{:S(2)}, u32[]{:S(2)}) %collective-permute-start.8) | collective-permute-done | bytes 65568 | tf_op jit(solution)/shard_map/ppermute | solution.py:349
  91.5 1.0 %all-to-all-done.3.grad_ref = bf16[16,16,256]{2,1,0:T(8,128)(2,1)S(1)} async-done(((bf16[16,16,256]{2,1,0:T(8,128)(2,1)}), bf16[16,16,256]{2,1,0:T(8,128)(2,1)S(1)}, u32[]{:S(2)}, u32[]{:S(2)}) %all-to-all-start.3) | async-done | bytes 131104 | tf_op jit(solution)/shard_map/all_to_all | solution.py:303
  92.5 1.0 %shard_map.77 = (f32[3,3,3,16,16]{4,3,2,1,0:T(8,128)}, f32[3,3,3,16,64]{4,3,2,1,0:T(8,128)}, bf16[16,1,64,128]{3,2,1,0:T(8,128)(2,1)}) custom-call(bf16[16,16,256]{2,1,0:T(8,128)(2,1)S(1)} %all-to-all-done.3.grad_ref, bf16[16,16,128]{2,1,0:T(8,128)(2,1)S(1)} %get-tuple-element.36.got0_ref, bf16[16,16,128]{2,1,0:T(8,128)(2,1)S(1)} %collective-permute-done.6.got1_ref, ...), custom_call_target="tpu_custom_call" | custom-call | flops 2000000000 | bytes 1000000 | tf_op jit(solution)/shard_map/pallas_call | solution.py:357
  (19 shorter events, 2.4 us)
Async XLA Ops:
  0.6 1.0 %copy-start = (bf16[16,2,32,256]{3,2,1,0:T(8,128)(2,1)S(1)}, bf16[16,2,32,256]{3,2,1,0:T(8,128)(2,1)}, u32[]{:S(2)}) copy-start(bf16[16,2,32,256]{3,2,1,0:T(8,128)(2,1)} %vol_hbm.1) | copy-start | bytes 1572868
  2.1 5.2 %collective-permute-start = (bf16[6,16,256]{2,1,0:T(8,128)(2,1)S(1)}, bf16[6,16,256]{2,1,0:T(8,128)(2,1)S(1)}, u32[]{:S(2)}, u32[]{:S(2)}) collective-permute-start(bf16[6,16,256]{2,1,0:T(8,128)(2,1)S(1)} %get-tuple-element.23.after_ref), channel_id=1, source_target_pairs={{0,1},{1,0},{2,3},{3,2},{4,5},{5,4},{6,7},{7,6},{8,9},{9,8},{10,11... | collective-permute-start | bytes 147464 | tf_op jit(solution)/shard_map/ppermute | solution.py:316
  5.4 5.4 %collective-permute-start.1 = (bf16[6,16,256]{2,1,0:T(8,128)(2,1)S(1)}, bf16[6,16,256]{2,1,0:T(8,128)(2,1)S(1)}, u32[]{:S(2)}, u32[]{:S(2)}) collective-permute-start(bf16[6,16,256]{2,1,0:T(8,128)(2,1)S(1)} %get-tuple-element.26), channel_id=1, source_target_pairs={{1,2},{2,1},{5,6},{6,5},{9,10},{10,9},{13,14},{14,13},{17,18},{18,... | collective-permute-start | bytes 147464 | tf_op jit(solution)/shard_map/ppermute | solution.py:317
  10.8 8.2 %copy-start.1 = (bf16[16,1,64,128]{3,2,1,0:T(8,128)(2,1)S(1)}, bf16[16,1,64,128]{3,2,1,0:T(8,128)(2,1)}, u32[]{:S(2)}) copy-start(bf16[16,1,64,128]{3,2,1,0:T(8,128)(2,1)} %cot_ref.1) | copy-start | bytes 786436
  10.8 12.9 %collective-permute-start.2 = (bf16[38,16,256]{2,1,0:T(8,128)(2,1)S(1)}, bf16[38,16,256]{2,1,0:T(8,128)(2,1)S(1)}, u32[]{:S(2)}, u32[]{:S(2)}) collective-permute-start(bf16[38,16,256]{2,1,0:T(8,128)(2,1)S(1)} %get-tuple-element.27.b_ref), channel_id=1, source_target_pairs={{4,8},{8,4},{12,16},{16,12},{20,24},{24,20},{28,32},{32,28},{36,40... | collective-permute-start | bytes 933896 | tf_op jit(solution)/shard_map/ppermute | solution.py:298
  11.6 11.8 %copy-start.2 = (bf16[16,16,3,3,3]{1,0,4,3,2:T(8,128)(2,1)S(1)}, bf16[16,16,3,3,3]{1,0,4,3,2:T(8,128)(2,1)}, u32[]{:S(2)}) copy-start(bf16[16,16,3,3,3]{1,0,4,3,2:T(8,128)(2,1)} %param.5) | copy-start | bytes 41476
  11.6 17.1 %collective-permute-start.3 = (bf16[38,16,256]{2,1,0:T(8,128)(2,1)S(1)}, bf16[38,16,256]{2,1,0:T(8,128)(2,1)S(1)}, u32[]{:S(2)}, u32[]{:S(2)}) collective-permute-start(bf16[38,16,256]{2,1,0:T(8,128)(2,1)S(1)} %get-tuple-element.28.c_ref), channel_id=1, source_target_pairs={{0,4},{4,0},{8,12},{12,8},{16,20},{20,16},{24,28},{28,24},{32,36},... | collective-permute-start | bytes 933896 | tf_op jit(solution)/shard_map/ppermute | solution.py:297
  19.9 10.9 %all-to-all-start = ((bf16[4,18,16,128]{3,2,1,0:T(8,128)(2,1)}), bf16[4,18,16,128]{3,2,1,0:T(8,128)(2,1)S(1)}, u32[]{:S(2)}, u32[]{:S(2)}) async-start(bf16[4,18,16,128]{3,2,1,0:T(8,128)(2,1)} %shard_map.68), calls=%async_computation | async-start | bytes 589824 | tf_op jit(solution)/shard_map/all_to_all | solution.py:318
  23.7 7.2 %copy-start.3 = (bf16[64,16,3,3,3]{0,1,4,3,2:T(8,128)(2,1)S(1)}, bf16[64,16,3,3,3]{0,1,4,3,2:T(8,128)(2,1)}, u32[]{:S(2)}) copy-start(bf16[64,16,3,3,3]{0,1,4,3,2:T(8,128)(2,1)} %param.6) | copy-start | bytes 165892
  31.6 8.5 %collective-permute-start.4 = (bf16[34,16,128]{2,1,0:T(8,128)(2,1)S(1)}, bf16[34,16,128]{2,1,0:T(8,128)(2,1)S(1)}, u32[]{:S(2)}, u32[]{:S(2)}) collective-permute-start(bf16[34,16,128]{2,1,0:T(8,128)(2,1)S(1)} %get-tuple-element.31.after_ref.own_msg), channel_id=1, source_target_pairs={{0,4},{4,0},{8,12},{12,8},{16,20},{20,16},{24,28},{28,24},{32,36},... | collective-permute-start | bytes 417800 | tf_op jit(solution)/shard_map/ppermute | solution.py:297
  33.7 6.5 %collective-permute-start.5 = (bf16[34,16,128]{2,1,0:T(8,128)(2,1)S(1)}, bf16[34,16,128]{2,1,0:T(8,128)(2,1)S(1)}, u32[]{:S(2)}, u32[]{:S(2)}) collective-permute-start(bf16[34,16,128]{2,1,0:T(8,128)(2,1)S(1)} %get-tuple-element.32), channel_id=1, source_target_pairs={{4,8},{8,4},{12,16},{16,12},{20,24},{24,20},{28,32},{32,28},{36,40... | collective-permute-start | bytes 417800 | tf_op jit(solution)/shard_map/ppermute | solution.py:298
  78.5 14.1 %all-to-all-start.3 = ((bf16[16,16,256]{2,1,0:T(8,128)(2,1)}), bf16[16,16,256]{2,1,0:T(8,128)(2,1)S(1)}, u32[]{:S(2)}, u32[]{:S(2)}) async-start(bf16[16,16,256]{2,1,0:T(8,128)(2,1)} %shard_map.76), calls=%async_computation.3 | async-start | bytes 262144 | tf_op jit(solution)/shard_map/all_to_all | solution.py:303
  83.1 2.1 %collective-permute-start.6 = (bf16[16,16,128]{2,1,0:T(8,128)(2,1)S(1)}, bf16[16,16,128]{2,1,0:T(8,128)(2,1)S(1)}, u32[]{:S(2)}, u32[]{:S(2)}) collective-permute-start(bf16[16,16,128]{2,1,0:T(8,128)(2,1)S(1)} %get-tuple-element.37), channel_id=1, source_target_pairs={{0,1},{1,0},{2,3},{3,2},{4,5},{5,4},{6,7},{7,6},{8,9},{9,8},{10,11... | collective-permute-start | bytes 196616 | tf_op jit(solution)/shard_map/ppermute | solution.py:349
  83.4 6.1 %collective-permute-start.7 = (bf16[16,16,128]{2,1,0:T(8,128)(2,1)S(1)}, bf16[16,16,128]{2,1,0:T(8,128)(2,1)S(1)}, u32[]{:S(2)}, u32[]{:S(2)}) collective-permute-start(bf16[16,16,128]{2,1,0:T(8,128)(2,1)S(1)} %get-tuple-element.38), channel_id=1, source_target_pairs={{0,2},{1,3},{2,0},{3,1},{4,6},{5,7},{6,4},{7,5},{8,10},{9,11},{10,... | collective-permute-start | bytes 196616 | tf_op jit(solution)/shard_map/ppermute | solution.py:349
  84.9 6.7 %collective-permute-start.8 = (bf16[16,16,128]{2,1,0:T(8,128)(2,1)S(1)}, bf16[16,16,128]{2,1,0:T(8,128)(2,1)S(1)}, u32[]{:S(2)}, u32[]{:S(2)}) collective-permute-start(bf16[16,16,128]{2,1,0:T(8,128)(2,1)S(1)} %get-tuple-element.39), channel_id=1, source_target_pairs={{0,3},{1,2},{2,1},{3,0},{4,7},{5,6},{6,5},{7,4},{8,11},{9,10},{10,... | collective-permute-start | bytes 196616 | tf_op jit(solution)/shard_map/ppermute | solution.py:349

commit v3 on v2

--- a/solution.py
+++ b/solution.py
@@ -351,9 +351,9 @@
     lines = [[16 * g + j for j in range(16)] for g in range(16)]
     sheets = [[16 * g + j for g in range(16)] for j in range(16)]
     summed = call(sum_kernel, [((16, 16, 256), BF16)])
-    parts = exchange(grads.reshape(16, 16, 256), lines)
-    parts = exchange(summed(parts)[0], sheets)
-    spread = exchange(summed(parts)[0], lines)
+    parts = exchange(grads.reshape(16, 16, 256), sheets)
+    parts = exchange(summed(parts)[0], lines)
+    spread = exchange(summed(parts)[0], sheets)
     grad_fine, grad_coarse, coarse_out = call(
         unpack_kernel, [((3, 3, 3, 16, 16), F32), ((3, 3, 3, 16, 64), F32), ((16, 1, 64, 128), BF16)], n_in=5
     )(spread, *out_got)

time: 94 us -> 91.5 us (0.973)
  waiting for transfers between devices: 22.1 us -> 19.3 us
  blocking collectives: 35.5 us -> 36.9 us
  starting transfers between devices: 26.2 us -> 25.2 us
    ppermute x3, waiting for transfers between devices: 6.29 us -> 3.62 us  [local(): lax.ppermute(out_pieces[k], 'fil', [(i, i ^ k) for i in range(4)])]
    all_to_all x2, blocking collectives: 35.5 us -> 36.9 us  [exchange(): lax.all_to_all(pieces, ('vox', 'fil'), 0, 0, tiled=True, axis_index_group...]
    all_to_all x1, starting transfers between devices: 4.65 us -> 3.51 us  [exchange(): lax.all_to_all(pieces, ('vox', 'fil'), 0, 0, tiled=True, axis_index_group...]
where the time goes in v3:
time: 91.5 us; the launch traced here: 91.1 us
  blocking collectives  36.9 us (40%)
  starting transfers between devices  25.2 us (28%)
  waiting for transfers between devices  19.3 us (21%)
  Pallas kernels  7.88 us (9%)
  local copies, waits for them, and re-layouts  1.05 us (1%)
    all_to_all x2, blocking collectives, exchange(): lax.all_to_all(pieces, ('vox', 'fil'), 0, 0, tiled=True, axis_index_group...  36.9 us
    ppermute x2, waiting for transfers between devices, swapped(): near = lax.ppermute(near, 'vox', first)  10.5 us
    ppermute x2, starting transfers between devices, swapped(): near = lax.ppermute(near, 'vox', first)  9.33 us
    ppermute x3, waiting for transfers between devices, local(): lax.ppermute(out_pieces[k], 'fil', [(i, i ^ k) for i in range(4)])  3.62 us
    all_to_all x1, starting transfers between devices, exchange(): lax.all_to_all(pieces, ('vox', 'fil'), 0, 0, tiled=True, axis_index_group...  3.51 us
    ppermute x1, waiting for transfers between devices, local(): edge3 = lax.ppermute(edge3, 'fil', [(1, 2), (2, 1)])  3.47 us
    all_to_all x1, starting transfers between devices, local(): got = lax.all_to_all(pay, 'fil', 0, 0, tiled=True)  3.44 us
    ppermute x1, starting transfers between devices, local(): edge1 = lax.ppermute(edge1, 'fil', [(i, i ^ 1) for i in range(4)])  3.29 us
  transfers between devices with their start and end apart: 11, of which 7 were waited for; matrix products, arithmetic and copies ran while one was open for 0% of the time, Pallas kernels for 3%

profile of v3, /device:TPU:1, one launch (start us, length us, event | category | flops | bytes accessed | tf_op | source)
XLA Modules:
  0.0 91.1 jit_solution(9622592163001000570)
XLA Ops:
  0.6 1.0 %copy-done = bf16[16,2,32,256]{3,2,1,0:T(8,128)(2,1)S(1)} copy-done((bf16[16,2,32,256]{3,2,1,0:T(8,128)(2,1)S(1)}, bf16[16,2,32,256]{3,2,1,0:T(8,128)(2,1)}, u32[]{:S(2)}) %copy-start) | copy-done | bytes 524312
  2.1 3.3 %collective-permute-start = (bf16[6,16,256]{2,1,0:T(8,128)(2,1)S(1)}, bf16[6,16,256]{2,1,0:T(8,128)(2,1)S(1)}, u32[]{:S(2)}, u32[]{:S(2)}) collective-permute-start(bf16[6,16,256]{2,1,0:T(8,128)(2,1)S(1)} %get-tuple-element.23.after_ref), channel_id=1, source_target_pairs={{0,1},{1,0},{2,3},{3,2},{4,5},{5,4},{6,7},{7,6},{8,9},{9,8},{10,11... | collective-permute-start | bytes 147464 | tf_op jit(solution)/shard_map/ppermute | solution.py:316
  5.4 1.9 %collective-permute-start.1 = (bf16[6,16,256]{2,1,0:T(8,128)(2,1)S(1)}, bf16[6,16,256]{2,1,0:T(8,128)(2,1)S(1)}, u32[]{:S(2)}, u32[]{:S(2)}) collective-permute-start(bf16[6,16,256]{2,1,0:T(8,128)(2,1)S(1)} %get-tuple-element.26), channel_id=1, source_target_pairs={{1,2},{2,1},{5,6},{6,5},{9,10},{10,9},{13,14},{14,13},{17,18},{18,... | collective-permute-start | bytes 147464 | tf_op jit(solution)/shard_map/ppermute | solution.py:317
  7.3 3.5 %collective-permute-done.1.edge3_ref = bf16[6,16,256]{2,1,0:T(8,128)(2,1)S(1)} collective-permute-done((bf16[6,16,256]{2,1,0:T(8,128)(2,1)S(1)}, bf16[6,16,256]{2,1,0:T(8,128)(2,1)S(1)}, u32[]{:S(2)}, u32[]{:S(2)}) %collective-permute-start.1) | collective-permute-done | bytes 49184 | tf_op jit(solution)/shard_map/ppermute | solution.py:317
  10.8 0.8 collective-permute-start.2
  11.6 7.3 %collective-permute-start.3 = (bf16[38,16,256]{2,1,0:T(8,128)(2,1)S(1)}, bf16[38,16,256]{2,1,0:T(8,128)(2,1)S(1)}, u32[]{:S(2)}, u32[]{:S(2)}) collective-permute-start(bf16[38,16,256]{2,1,0:T(8,128)(2,1)S(1)} %get-tuple-element.28.c_ref), channel_id=1, source_target_pairs={{0,4},{4,0},{8,12},{12,8},{16,20},{20,16},{24,28},{28,24},{32,36},... | collective-permute-start | bytes 933896 | tf_op jit(solution)/shard_map/ppermute | solution.py:297
  18.9 1.0 %shard_map.68 = bf16[4,18,16,128]{3,2,1,0:T(8,128)(2,1)} custom-call(bf16[16,1,64,128]{3,2,1,0:T(8,128)(2,1)S(1)} %copy-done.1, bf16[6,16,256]{2,1,0:T(8,128)(2,1)S(1)} %get-tuple-element.23.after_ref), custom_call_target="tpu_custom_call" | custom-call | flops 2000000000 | bytes 1000000 | tf_op jit(solution)/shard_map/pallas_call | solution.py:315
  19.9 3.4 %all-to-all-start = ((bf16[4,18,16,128]{3,2,1,0:T(8,128)(2,1)}), bf16[4,18,16,128]{3,2,1,0:T(8,128)(2,1)S(1)}, u32[]{:S(2)}, u32[]{:S(2)}) async-start(bf16[4,18,16,128]{3,2,1,0:T(8,128)(2,1)} %shard_map.68), calls=%async_computation | async-start | bytes 589824 | tf_op jit(solution)/shard_map/all_to_all | solution.py:318
  23.7 5.0 %collective-permute-done.3.d_ref = bf16[38,16,256]{2,1,0:T(8,128)(2,1)S(1)} collective-permute-done((bf16[38,16,256]{2,1,0:T(8,128)(2,1)S(1)}, bf16[38,16,256]{2,1,0:T(8,128)(2,1)S(1)}, u32[]{:S(2)}, u32[]{:S(2)}) %collective-permute-start.3) | collective-permute-done | bytes 311328 | tf_op jit(solution)/shard_map/ppermute | solution.py:297
  28.7 1.3 %shard_map.71 = (bf16[18,16,128]{2,1,0:T(8,128)(2,1)S(1)}, bf16[16,64,256]{2,1,0:T(8,128)(2,1)S(1)}, bf16[4,38,16,256]{3,2,1,0:T(8,128)(2,1)S(1)}) custom-call(bf16[38,16,256]{2,1,0:T(8,128)(2,1)S(1)} %collective-permute-done.2.a_ref, bf16[38,16,256]{2,1,0:T(8,128)(2,1)S(1)} %get-tuple-element.27.b_ref, bf16[38,16,256]{2,1,0:T(8,128)(2,1)S(1)} %get-tuple-element.28.c_ref, ...), custom_call_target="tpu_custom_call" | custom-call | flops 2000000000 | bytes 1000000 | tf_op jit(solution)/shard_map/pallas_call | solution.py:323
  30.0 0.9 all-to-all-done.got_ref
  30.9 0.7 shard_map.72
  31.6 2.0 %collective-permute-start.4 = (bf16[34,16,128]{2,1,0:T(8,128)(2,1)S(1)}, bf16[34,16,128]{2,1,0:T(8,128)(2,1)S(1)}, u32[]{:S(2)}, u32[]{:S(2)}) collective-permute-start(bf16[34,16,128]{2,1,0:T(8,128)(2,1)S(1)} %get-tuple-element.31.after_ref.own_msg), channel_id=1, source_target_pairs={{0,4},{4,0},{8,12},{12,8},{16,20},{20,16},{24,28},{28,24},{32,36},... | collective-permute-start | bytes 417800 | tf_op jit(solution)/shard_map/ppermute | solution.py:297
  34.6 5.5 %collective-permute-done.4.near_msg = bf16[34,16,128]{2,1,0:T(8,128)(2,1)S(1)} collective-permute-done((bf16[34,16,128]{2,1,0:T(8,128)(2,1)S(1)}, bf16[34,16,128]{2,1,0:T(8,128)(2,1)S(1)}, u32[]{:S(2)}, u32[]{:S(2)}) %collective-permute-start.4) | collective-permute-done | bytes 139296 | tf_op jit(solution)/shard_map/ppermute | solution.py:297
  40.1 2.1 %shard_map.74 = (bf16[16,16,128]{2,1,0:T(8,128)(2,1)S(1)}, bf16[16,16,128]{2,1,0:T(8,128)(2,1)S(1)}, bf16[16,16,128]{2,1,0:T(8,128)(2,1)S(1)}, bf16[16,16,128]{2,1,0:T(8,128)(2,1)S(1)}, bf16[256,256]{1,0:T(8,128)(2,1)S(1)}) custom-call(f32[16,16,128]{2,1,0:T(8,128)S(1)} %get-tuple-element.30.own_r, bf16[34,16,128]{2,1,0:T(8,128)(2,1)S(1)} %collective-permute-done.4.near_msg, ...), custom_call_target="tpu_custom_call" | custom-call | flops 2000000000 | bytes 1000000 | tf_op jit(solution)/shard_map/pallas_call | solution.py:335
  42.2 18.3 %all_to_all.20.parts_ref = bf16[16,16,256]{2,1,0:T(8,128)(2,1)S(1)} all-to-all(bf16[16,16,256]{2,1,0:T(8,128)(2,1)S(1)} %bitcast.5), channel_id=1, replica_groups={{0,16,32,48,64,80,96,112,128,144,160,176,192,208,224,240},{1,17,33,49,6..., dimensions={0} | all-to-all | bytes 262144 | tf_op jit(solution)/shard_map/all_to_all | solution.py:303
  60.6 18.5 %all_to_all.21.parts_ref = bf16[16,16,256]{2,1,0:T(8,128)(2,1)S(1)} all-to-all(bf16[16,16,256]{2,1,0:T(8,128)(2,1)S(1)} %shard_map.75), channel_id=1, replica_groups={{0,1,2,3,4,5,6,7,8,9,10,11,12,13,14,15},{16,17,18,19,20,21,22,23,24,25,..., dimensions={0} | all-to-all | bytes 262144 | tf_op jit(solution)/shard_map/all_to_all | solution.py:303
  79.1 0.7 shard_map.76
  79.8 3.5 %all-to-all-start.3 = ((bf16[16,16,256]{2,1,0:T(8,128)(2,1)}), bf16[16,16,256]{2,1,0:T(8,128)(2,1)S(1)}, u32[]{:S(2)}, u32[]{:S(2)}) async-start(bf16[16,16,256]{2,1,0:T(8,128)(2,1)} %shard_map.76), calls=%async_computation.3 | async-start | bytes 262144 | tf_op jit(solution)/shard_map/all_to_all | solution.py:303
  83.8 1.8 %collective-permute-start.8 = (bf16[16,16,128]{2,1,0:T(8,128)(2,1)S(1)}, bf16[16,16,128]{2,1,0:T(8,128)(2,1)S(1)}, u32[]{:S(2)}, u32[]{:S(2)}) collective-permute-start(bf16[16,16,128]{2,1,0:T(8,128)(2,1)S(1)} %get-tuple-element.39), channel_id=1, source_target_pairs={{0,3},{1,2},{2,1},{3,0},{4,7},{5,6},{6,5},{7,4},{8,11},{9,10},{10,... | collective-permute-start | bytes 196616 | tf_op jit(solution)/shard_map/ppermute | solution.py:349
  85.6 1.4 %collective-permute-done.7.got2_ref = bf16[16,16,128]{2,1,0:T(8,128)(2,1)S(1)} collective-permute-done((bf16[16,16,128]{2,1,0:T(8,128)(2,1)S(1)}, bf16[16,16,128]{2,1,0:T(8,128)(2,1)S(1)}, u32[]{:S(2)}, u32[]{:S(2)}) %collective-permute-start.7) | collective-permute-done | bytes 65568 | tf_op jit(solution)/shard_map/ppermute | solution.py:349
  86.9 2.3 %collective-permute-done.8.got3_ref = bf16[16,16,128]{2,1,0:T(8,128)(2,1)S(1)} collective-permute-done((bf16[16,16,128]{2,1,0:T(8,128)(2,1)S(1)}, bf16[16,16,128]{2,1,0:T(8,128)(2,1)S(1)}, u32[]{:S(2)}, u32[]{:S(2)}) %collective-permute-start.8) | collective-permute-done | bytes 65568 | tf_op jit(solution)/shard_map/ppermute | solution.py:349
  89.2 0.9 all-to-all-done.3.grad_ref
  90.0 1.0 %shard_map.77 = (f32[3,3,3,16,16]{4,3,2,1,0:T(8,128)}, f32[3,3,3,16,64]{4,3,2,1,0:T(8,128)}, bf16[16,1,64,128]{3,2,1,0:T(8,128)(2,1)}) custom-call(bf16[16,16,256]{2,1,0:T(8,128)(2,1)S(1)} %all-to-all-done.3.grad_ref, bf16[16,16,128]{2,1,0:T(8,128)(2,1)S(1)} %get-tuple-element.36.got0_ref, bf16[16,16,128]{2,1,0:T(8,128)(2,1)S(1)} %collective-permute-done.6.got1_ref, ...), custom_call_target="tpu_custom_call" | custom-call | flops 2000000000 | bytes 1000000 | tf_op jit(solution)/shard_map/pallas_call | solution.py:357
  (19 shorter events, 2.2 us)
Async XLA Ops:
  0.6 1.0 %copy-start = (bf16[16,2,32,256]{3,2,1,0:T(8,128)(2,1)S(1)}, bf16[16,2,32,256]{3,2,1,0:T(8,128)(2,1)}, u32[]{:S(2)}) copy-start(bf16[16,2,32,256]{3,2,1,0:T(8,128)(2,1)} %vol_hbm.1) | copy-start | bytes 1572868
  2.1 5.2 %collective-permute-start = (bf16[6,16,256]{2,1,0:T(8,128)(2,1)S(1)}, bf16[6,16,256]{2,1,0:T(8,128)(2,1)S(1)}, u32[]{:S(2)}, u32[]{:S(2)}) collective-permute-start(bf16[6,16,256]{2,1,0:T(8,128)(2,1)S(1)} %get-tuple-element.23.after_ref), channel_id=1, source_target_pairs={{0,1},{1,0},{2,3},{3,2},{4,5},{5,4},{6,7},{7,6},{8,9},{9,8},{10,11... | collective-permute-start | bytes 147464 | tf_op jit(solution)/shard_map/ppermute | solution.py:316
  5.4 5.4 %collective-permute-start.1 = (bf16[6,16,256]{2,1,0:T(8,128)(2,1)S(1)}, bf16[6,16,256]{2,1,0:T(8,128)(2,1)S(1)}, u32[]{:S(2)}, u32[]{:S(2)}) collective-permute-start(bf16[6,16,256]{2,1,0:T(8,128)(2,1)S(1)} %get-tuple-element.26), channel_id=1, source_target_pairs={{1,2},{2,1},{5,6},{6,5},{9,10},{10,9},{13,14},{14,13},{17,18},{18,... | collective-permute-start | bytes 147464 | tf_op jit(solution)/shard_map/ppermute | solution.py:317
  10.8 8.2 %copy-start.1 = (bf16[16,1,64,128]{3,2,1,0:T(8,128)(2,1)S(1)}, bf16[16,1,64,128]{3,2,1,0:T(8,128)(2,1)}, u32[]{:S(2)}) copy-start(bf16[16,1,64,128]{3,2,1,0:T(8,128)(2,1)} %cot_ref.1) | copy-start | bytes 786436
  10.8 12.9 %collective-permute-start.2 = (bf16[38,16,256]{2,1,0:T(8,128)(2,1)S(1)}, bf16[38,16,256]{2,1,0:T(8,128)(2,1)S(1)}, u32[]{:S(2)}, u32[]{:S(2)}) collective-permute-start(bf16[38,16,256]{2,1,0:T(8,128)(2,1)S(1)} %get-tuple-element.27.b_ref), channel_id=1, source_target_pairs={{4,8},{8,4},{12,16},{16,12},{20,24},{24,20},{28,32},{32,28},{36,40... | collective-permute-start | bytes 933896 | tf_op jit(solution)/shard_map/ppermute | solution.py:298
  11.6 11.8 %copy-start.2 = (bf16[16,16,3,3,3]{1,0,4,3,2:T(8,128)(2,1)S(1)}, bf16[16,16,3,3,3]{1,0,4,3,2:T(8,128)(2,1)}, u32[]{:S(2)}) copy-start(bf16[16,16,3,3,3]{1,0,4,3,2:T(8,128)(2,1)} %param.5) | copy-start | bytes 41476
  11.6 17.1 %collective-permute-start.3 = (bf16[38,16,256]{2,1,0:T(8,128)(2,1)S(1)}, bf16[38,16,256]{2,1,0:T(8,128)(2,1)S(1)}, u32[]{:S(2)}, u32[]{:S(2)}) collective-permute-start(bf16[38,16,256]{2,1,0:T(8,128)(2,1)S(1)} %get-tuple-element.28.c_ref), channel_id=1, source_target_pairs={{0,4},{4,0},{8,12},{12,8},{16,20},{20,16},{24,28},{28,24},{32,36},... | collective-permute-start | bytes 933896 | tf_op jit(solution)/shard_map/ppermute | solution.py:297
  19.9 10.9 %all-to-all-start = ((bf16[4,18,16,128]{3,2,1,0:T(8,128)(2,1)}), bf16[4,18,16,128]{3,2,1,0:T(8,128)(2,1)S(1)}, u32[]{:S(2)}, u32[]{:S(2)}) async-start(bf16[4,18,16,128]{3,2,1,0:T(8,128)(2,1)} %shard_map.68), calls=%async_computation | async-start | bytes 589824 | tf_op jit(solution)/shard_map/all_to_all | solution.py:318
  23.7 7.2 %copy-start.3 = (bf16[64,16,3,3,3]{0,1,4,3,2:T(8,128)(2,1)S(1)}, bf16[64,16,3,3,3]{0,1,4,3,2:T(8,128)(2,1)}, u32[]{:S(2)}) copy-start(bf16[64,16,3,3,3]{0,1,4,3,2:T(8,128)(2,1)} %param.6) | copy-start | bytes 165892
  31.6 8.5 %collective-permute-start.4 = (bf16[34,16,128]{2,1,0:T(8,128)(2,1)S(1)}, bf16[34,16,128]{2,1,0:T(8,128)(2,1)S(1)}, u32[]{:S(2)}, u32[]{:S(2)}) collective-permute-start(bf16[34,16,128]{2,1,0:T(8,128)(2,1)S(1)} %get-tuple-element.31.after_ref.own_msg), channel_id=1, source_target_pairs={{0,4},{4,0},{8,12},{12,8},{16,20},{20,16},{24,28},{28,24},{32,36},... | collective-permute-start | bytes 417800 | tf_op jit(solution)/shard_map/ppermute | solution.py:297
  33.7 6.5 %collective-permute-start.5 = (bf16[34,16,128]{2,1,0:T(8,128)(2,1)S(1)}, bf16[34,16,128]{2,1,0:T(8,128)(2,1)S(1)}, u32[]{:S(2)}, u32[]{:S(2)}) collective-permute-start(bf16[34,16,128]{2,1,0:T(8,128)(2,1)S(1)} %get-tuple-element.32), channel_id=1, source_target_pairs={{4,8},{8,4},{12,16},{16,12},{20,24},{24,20},{28,32},{32,28},{36,40... | collective-permute-start | bytes 417800 | tf_op jit(solution)/shard_map/ppermute | solution.py:298
  79.8 10.2 %all-to-all-start.3 = ((bf16[16,16,256]{2,1,0:T(8,128)(2,1)}), bf16[16,16,256]{2,1,0:T(8,128)(2,1)S(1)}, u32[]{:S(2)}, u32[]{:S(2)}) async-start(bf16[16,16,256]{2,1,0:T(8,128)(2,1)} %shard_map.76), calls=%async_computation.3 | async-start | bytes 262144 | tf_op jit(solution)/shard_map/all_to_all | solution.py:303
  83.3 2.2 %collective-permute-start.6 = (bf16[16,16,128]{2,1,0:T(8,128)(2,1)S(1)}, bf16[16,16,128]{2,1,0:T(8,128)(2,1)S(1)}, u32[]{:S(2)}, u32[]{:S(2)}) collective-permute-start(bf16[16,16,128]{2,1,0:T(8,128)(2,1)S(1)} %get-tuple-element.37), channel_id=1, source_target_pairs={{0,1},{1,0},{2,3},{3,2},{4,5},{5,4},{6,7},{7,6},{8,9},{9,8},{10,11... | collective-permute-start | bytes 196616 | tf_op jit(solution)/shard_map/ppermute | solution.py:349
  83.4 3.5 %collective-permute-start.7 = (bf16[16,16,128]{2,1,0:T(8,128)(2,1)S(1)}, bf16[16,16,128]{2,1,0:T(8,128)(2,1)S(1)}, u32[]{:S(2)}, u32[]{:S(2)}) collective-permute-start(bf16[16,16,128]{2,1,0:T(8,128)(2,1)S(1)} %get-tuple-element.38), channel_id=1, source_target_pairs={{0,2},{1,3},{2,0},{3,1},{4,6},{5,7},{6,4},{7,5},{8,10},{9,11},{10,... | collective-permute-start | bytes 196616 | tf_op jit(solution)/shard_map/ppermute | solution.py:349
  83.8 5.4 %collective-permute-start.8 = (bf16[16,16,128]{2,1,0:T(8,128)(2,1)S(1)}, bf16[16,16,128]{2,1,0:T(8,128)(2,1)S(1)}, u32[]{:S(2)}, u32[]{:S(2)}) collective-permute-start(bf16[16,16,128]{2,1,0:T(8,128)(2,1)S(1)} %get-tuple-element.39), channel_id=1, source_target_pairs={{0,3},{1,2},{2,1},{3,0},{4,7},{5,6},{6,5},{7,4},{8,11},{9,10},{10,... | collective-permute-start | bytes 196616 | tf_op jit(solution)/shard_map/ppermute | solution.py:349

commit v4 on v3

--- a/solution.py
+++ b/solution.py
@@ -211,17 +211,14 @@
     scaled = (total * 0.125).astype(BF16).reshape(256, 128)
     spread = jnp.where(iota((128, 256), 0) == iota((128, 256), 1) // 2, 1.0, 0.0).astype(BF16)
     up[...] = dot(scaled, spread).reshape(16, 16, 256)
-    acc[...] = jnp.zeros_like(acc)
-
-    def step(y, carry):
-        row = up[y]
-        cot = jnp.concatenate([row] * 4, 0) * mask_ref[y].astype(F32)
-        left = jnp.concatenate([moved(cot, -1), cot, moved(cot, 1)], 0).astype(BF16)
-        window = window_of(planes_of(all_ref), 2 * y + 2, 4)
-        acc[...] += dot_t(left, window)
-        return carry
-
-    lax.fori_loop(0, 16, step, 0, unroll=True)
+    for group in range(4):
+        lefts, windows = [], []
+        for y in range(4 * group, 4 * group + 4):
+            cot = jnp.concatenate([up[y]] * 4, 0) * mask_ref[y].astype(F32)
+            lefts.append(jnp.concatenate([moved(cot, -1), cot, moved(cot, 1)], 0).astype(BF16))
+            windows.append(window_of(planes_of(all_ref), 2 * y + 2, 4))
+        part = dot_t(jnp.concatenate(lefts, 1), jnp.concatenate(windows, 1))
+        acc[...] = part if group == 0 else acc[...] + part
     for t in range(3):
         total = None
         for cell in range(4):
@@ -239,22 +236,21 @@
     slab[2 - 2 * odd] = near_msg[0:18]
     slab[1] = own_msg[0:18]
     slab[2 * odd] = far_msg[0:18]
-    acc[...] = jnp.zeros_like(acc)
     pad = jnp.zeros((64, 128), BF16)
-
-    def step(pair, carry):
-        window = jnp.concatenate([window_of([slab.at[x] for x in range(3)], 2 * pair, 3), pad], 0)
-        product = dot(w4_ref[...], window)
-        result = moved(product[0:128], 1) + product[128:256] + moved(product[256:384], -1)
-        result = result.astype(BF16).reshape(2, 4, 16, 128)
-        for dest in range(4):
-            rows_out[dest, pl.ds(2 * pair, 2)] = result[:, dest]
-        cot = jnp.concatenate([got_ref[:, 2 * pair + 1 + s].reshape(64, 128) for s in range(2)], 0).astype(F32)
-        left = jnp.concatenate([moved(cot, -1), cot, moved(cot, 1)], 0).astype(BF16)
-        acc[...] += dot_t(left, window)
-        return carry
-
-    lax.fori_loop(0, 8, step, 0, unroll=True)
+    for group in range(2):
+        lefts, windows = [], []
+        for pair in range(4 * group, 4 * group + 4):
+            window = jnp.concatenate([window_of([slab.at[x] for x in range(3)], 2 * pair, 3), pad], 0)
+            product = dot(w4_ref[...], window)
+            result = moved(product[0:128], 1) + product[128:256] + moved(product[256:384], -1)
+            result = result.astype(BF16).reshape(2, 4, 16, 128)
+            for dest in range(4):
+                rows_out[dest, 2 * pair : 2 * pair + 2] = result[:, dest]
+            cot = jnp.concatenate([got_ref[:, 2 * pair + 1 + s].reshape(64, 128) for s in range(2)], 0).astype(F32)
+            lefts.append(jnp.concatenate([moved(cot, -1), cot, moved(cot, 1)], 0).astype(BF16))
+            windows.append(window)
+        part = dot_t(jnp.concatenate(lefts, 1), jnp.concatenate(windows, 1))
+        acc[...] = part if group == 0 else acc[...] + part
     swap = swap_matrix()
     for k, out_ref in enumerate((out0_ref, out1_ref, out2_ref, out3_ref)):
         block = rows_out[lax.bitwise_xor(fil, k)].reshape(256, 128)

time: 91.5 us -> 91.2 us (level)
  no operation moved by 1% of the time
where the time goes in v4:
time: 91.2 us; the launch traced here: 90.7 us
  blocking collectives  36.9 us (40%)
  starting transfers between devices  25.2 us (28%)
  waiting for transfers between devices  19.3 us (21%)
  Pallas kernels  7.5 us (8%)
  local copies, waits for them, and re-layouts  1.05 us (1%)
    all_to_all x2, blocking collectives, exchange(): lax.all_to_all(pieces, ('vox', 'fil'), 0, 0, tiled=True, axis_index_group...  36.9 us
    ppermute x2, waiting for transfers between devices, swapped(): near = lax.ppermute(near, 'vox', first)  10.5 us
    ppermute x2, starting transfers between devices, swapped(): near = lax.ppermute(near, 'vox', first)  9.33 us
    ppermute x3, waiting for transfers between devices, local(): lax.ppermute(out_pieces[k], 'fil', [(i, i ^ k) for i in range(4)])  3.62 us
    all_to_all x1, starting transfers between devices, exchange(): lax.all_to_all(pieces, ('vox', 'fil'), 0, 0, tiled=True, axis_index_group...  3.51 us
    ppermute x1, waiting for transfers between devices, local(): edge3 = lax.ppermute(edge3, 'fil', [(1, 2), (2, 1)])  3.47 us
    all_to_all x1, starting transfers between devices, local(): got = lax.all_to_all(pay, 'fil', 0, 0, tiled=True)  3.44 us
    ppermute x1, starting transfers between devices, local(): edge1 = lax.ppermute(edge1, 'fil', [(i, i ^ 1) for i in range(4)])  3.29 us
  transfers between devices with their start and end apart: 11, of which 7 were waited for; matrix products, arithmetic and copies ran while one was open for 0% of the time, Pallas kernels for 3%

profile of v4, /device:TPU:1, one launch (start us, length us, event | category | flops | bytes accessed | tf_op | source)
XLA Modules:
  0.0 90.7 jit_solution(719518246215938687)
XLA Ops:
  0.6 1.0 %copy-done = bf16[16,2,32,256]{3,2,1,0:T(8,128)(2,1)S(1)} copy-done((bf16[16,2,32,256]{3,2,1,0:T(8,128)(2,1)S(1)}, bf16[16,2,32,256]{3,2,1,0:T(8,128)(2,1)}, u32[]{:S(2)}) %copy-start) | copy-done | bytes 524312
  2.1 3.3 %collective-permute-start = (bf16[6,16,256]{2,1,0:T(8,128)(2,1)S(1)}, bf16[6,16,256]{2,1,0:T(8,128)(2,1)S(1)}, u32[]{:S(2)}, u32[]{:S(2)}) collective-permute-start(bf16[6,16,256]{2,1,0:T(8,128)(2,1)S(1)} %get-tuple-element.23.after_ref), channel_id=1, source_target_pairs={{0,1},{1,0},{2,3},{3,2},{4,5},{5,4},{6,7},{7,6},{8,9},{9,8},{10,11... | collective-permute-start | bytes 147464 | tf_op jit(solution)/shard_map/ppermute | solution.py:312
  5.4 1.9 %collective-permute-start.1 = (bf16[6,16,256]{2,1,0:T(8,128)(2,1)S(1)}, bf16[6,16,256]{2,1,0:T(8,128)(2,1)S(1)}, u32[]{:S(2)}, u32[]{:S(2)}) collective-permute-start(bf16[6,16,256]{2,1,0:T(8,128)(2,1)S(1)} %get-tuple-element.26), channel_id=1, source_target_pairs={{1,2},{2,1},{5,6},{6,5},{9,10},{10,9},{13,14},{14,13},{17,18},{18,... | collective-permute-start | bytes 147464 | tf_op jit(solution)/shard_map/ppermute | solution.py:313
  7.3 3.5 %collective-permute-done.1.edge3_ref = bf16[6,16,256]{2,1,0:T(8,128)(2,1)S(1)} collective-permute-done((bf16[6,16,256]{2,1,0:T(8,128)(2,1)S(1)}, bf16[6,16,256]{2,1,0:T(8,128)(2,1)S(1)}, u32[]{:S(2)}, u32[]{:S(2)}) %collective-permute-start.1) | collective-permute-done | bytes 49184 | tf_op jit(solution)/shard_map/ppermute | solution.py:313
  10.8 0.8 collective-permute-start.2
  11.6 7.3 %collective-permute-start.3 = (bf16[38,16,256]{2,1,0:T(8,128)(2,1)S(1)}, bf16[38,16,256]{2,1,0:T(8,128)(2,1)S(1)}, u32[]{:S(2)}, u32[]{:S(2)}) collective-permute-start(bf16[38,16,256]{2,1,0:T(8,128)(2,1)S(1)} %get-tuple-element.28.c_ref), channel_id=1, source_target_pairs={{0,4},{4,0},{8,12},{12,8},{16,20},{20,16},{24,28},{28,24},{32,36},... | collective-permute-start | bytes 933896 | tf_op jit(solution)/shard_map/ppermute | solution.py:293
  18.9 1.0 %shard_map.68 = bf16[4,18,16,128]{3,2,1,0:T(8,128)(2,1)} custom-call(bf16[16,1,64,128]{3,2,1,0:T(8,128)(2,1)S(1)} %copy-done.1, bf16[6,16,256]{2,1,0:T(8,128)(2,1)S(1)} %get-tuple-element.23.after_ref), custom_call_target="tpu_custom_call" | custom-call | flops 2000000000 | bytes 1000000 | tf_op jit(solution)/shard_map/pallas_call | solution.py:311
  19.9 3.4 %all-to-all-start = ((bf16[4,18,16,128]{3,2,1,0:T(8,128)(2,1)}), bf16[4,18,16,128]{3,2,1,0:T(8,128)(2,1)S(1)}, u32[]{:S(2)}, u32[]{:S(2)}) async-start(bf16[4,18,16,128]{3,2,1,0:T(8,128)(2,1)} %shard_map.68), calls=%async_computation | async-start | bytes 589824 | tf_op jit(solution)/shard_map/all_to_all | solution.py:314
  23.7 5.0 %collective-permute-done.3.d_ref = bf16[38,16,256]{2,1,0:T(8,128)(2,1)S(1)} collective-permute-done((bf16[38,16,256]{2,1,0:T(8,128)(2,1)S(1)}, bf16[38,16,256]{2,1,0:T(8,128)(2,1)S(1)}, u32[]{:S(2)}, u32[]{:S(2)}) %collective-permute-start.3) | collective-permute-done | bytes 311328 | tf_op jit(solution)/shard_map/ppermute | solution.py:293
  28.7 1.3 %shard_map.71 = (bf16[18,16,128]{2,1,0:T(8,128)(2,1)S(1)}, bf16[16,64,256]{2,1,0:T(8,128)(2,1)S(1)}, bf16[4,38,16,256]{3,2,1,0:T(8,128)(2,1)S(1)}) custom-call(bf16[38,16,256]{2,1,0:T(8,128)(2,1)S(1)} %collective-permute-done.2.a_ref, bf16[38,16,256]{2,1,0:T(8,128)(2,1)S(1)} %get-tuple-element.27.b_ref, bf16[38,16,256]{2,1,0:T(8,128)(2,1)S(1)} %get-tuple-element.28.c_ref, ...), custom_call_target="tpu_custom_call" | custom-call | flops 2000000000 | bytes 1000000 | tf_op jit(solution)/shard_map/pallas_call | solution.py:319
  30.0 0.9 all-to-all-done.got_ref
  30.9 0.7 shard_map.72
  31.6 2.0 %collective-permute-start.4 = (bf16[34,16,128]{2,1,0:T(8,128)(2,1)S(1)}, bf16[34,16,128]{2,1,0:T(8,128)(2,1)S(1)}, u32[]{:S(2)}, u32[]{:S(2)}) collective-permute-start(bf16[34,16,128]{2,1,0:T(8,128)(2,1)S(1)} %get-tuple-element.31.after_ref.own_msg), channel_id=1, source_target_pairs={{0,4},{4,0},{8,12},{12,8},{16,20},{20,16},{24,28},{28,24},{32,36},... | collective-permute-start | bytes 417800 | tf_op jit(solution)/shard_map/ppermute | solution.py:293
  34.6 5.5 %collective-permute-done.4.near_msg = bf16[34,16,128]{2,1,0:T(8,128)(2,1)S(1)} collective-permute-done((bf16[34,16,128]{2,1,0:T(8,128)(2,1)S(1)}, bf16[34,16,128]{2,1,0:T(8,128)(2,1)S(1)}, u32[]{:S(2)}, u32[]{:S(2)}) %collective-permute-start.4) | collective-permute-done | bytes 139296 | tf_op jit(solution)/shard_map/ppermute | solution.py:293
  40.1 1.7 %shard_map.74 = (bf16[16,16,128]{2,1,0:T(8,128)(2,1)S(1)}, bf16[16,16,128]{2,1,0:T(8,128)(2,1)S(1)}, bf16[16,16,128]{2,1,0:T(8,128)(2,1)S(1)}, bf16[16,16,128]{2,1,0:T(8,128)(2,1)S(1)}, bf16[256,256]{1,0:T(8,128)(2,1)S(1)}) custom-call(f32[16,16,128]{2,1,0:T(8,128)S(1)} %get-tuple-element.30.own_r, bf16[34,16,128]{2,1,0:T(8,128)(2,1)S(1)} %collective-permute-done.4.near_msg, ...), custom_call_target="tpu_custom_call" | custom-call | flops 2000000000 | bytes 1000000 | tf_op jit(solution)/shard_map/pallas_call | solution.py:331
  41.9 18.3 %all_to_all.20.parts_ref = bf16[16,16,256]{2,1,0:T(8,128)(2,1)S(1)} all-to-all(bf16[16,16,256]{2,1,0:T(8,128)(2,1)S(1)} %bitcast.5), channel_id=1, replica_groups={{0,16,32,48,64,80,96,112,128,144,160,176,192,208,224,240},{1,17,33,49,6..., dimensions={0} | all-to-all | bytes 262144 | tf_op jit(solution)/shard_map/all_to_all | solution.py:299
  60.2 18.5 %all_to_all.21.parts_ref = bf16[16,16,256]{2,1,0:T(8,128)(2,1)S(1)} all-to-all(bf16[16,16,256]{2,1,0:T(8,128)(2,1)S(1)} %shard_map.75), channel_id=1, replica_groups={{0,1,2,3,4,5,6,7,8,9,10,11,12,13,14,15},{16,17,18,19,20,21,22,23,24,25,..., dimensions={0} | all-to-all | bytes 262144 | tf_op jit(solution)/shard_map/all_to_all | solution.py:299
  78.8 0.7 shard_map.76
  79.4 3.5 %all-to-all-start.3 = ((bf16[16,16,256]{2,1,0:T(8,128)(2,1)}), bf16[16,16,256]{2,1,0:T(8,128)(2,1)S(1)}, u32[]{:S(2)}, u32[]{:S(2)}) async-start(bf16[16,16,256]{2,1,0:T(8,128)(2,1)} %shard_map.76), calls=%async_computation.3 | async-start | bytes 262144 | tf_op jit(solution)/shard_map/all_to_all | solution.py:299
  83.4 1.8 %collective-permute-start.8 = (bf16[16,16,128]{2,1,0:T(8,128)(2,1)S(1)}, bf16[16,16,128]{2,1,0:T(8,128)(2,1)S(1)}, u32[]{:S(2)}, u32[]{:S(2)}) collective-permute-start(bf16[16,16,128]{2,1,0:T(8,128)(2,1)S(1)} %get-tuple-element.39), channel_id=1, source_target_pairs={{0,3},{1,2},{2,1},{3,0},{4,7},{5,6},{6,5},{7,4},{8,11},{9,10},{10,... | collective-permute-start | bytes 196616 | tf_op jit(solution)/shard_map/ppermute | solution.py:345
  85.2 1.4 %collective-permute-done.7.got2_ref = bf16[16,16,128]{2,1,0:T(8,128)(2,1)S(1)} collective-permute-done((bf16[16,16,128]{2,1,0:T(8,128)(2,1)S(1)}, bf16[16,16,128]{2,1,0:T(8,128)(2,1)S(1)}, u32[]{:S(2)}, u32[]{:S(2)}) %collective-permute-start.7) | collective-permute-done | bytes 65568 | tf_op jit(solution)/shard_map/ppermute | solution.py:345
  86.6 2.3 %collective-permute-done.8.got3_ref = bf16[16,16,128]{2,1,0:T(8,128)(2,1)S(1)} collective-permute-done((bf16[16,16,128]{2,1,0:T(8,128)(2,1)S(1)}, bf16[16,16,128]{2,1,0:T(8,128)(2,1)S(1)}, u32[]{:S(2)}, u32[]{:S(2)}) %collective-permute-start.8) | collective-permute-done | bytes 65568 | tf_op jit(solution)/shard_map/ppermute | solution.py:345
  88.8 0.9 all-to-all-done.3.grad_ref
  89.7 1.0 %shard_map.77 = (f32[3,3,3,16,16]{4,3,2,1,0:T(8,128)}, f32[3,3,3,16,64]{4,3,2,1,0:T(8,128)}, bf16[16,1,64,128]{3,2,1,0:T(8,128)(2,1)}) custom-call(bf16[16,16,256]{2,1,0:T(8,128)(2,1)S(1)} %all-to-all-done.3.grad_ref, bf16[16,16,128]{2,1,0:T(8,128)(2,1)S(1)} %get-tuple-element.36.got0_ref, bf16[16,16,128]{2,1,0:T(8,128)(2,1)S(1)} %collective-permute-done.6.got1_ref, ...), custom_call_target="tpu_custom_call" | custom-call | flops 2000000000 | bytes 1000000 | tf_op jit(solution)/shard_map/pallas_call | solution.py:353
  (19 shorter events, 2.2 us)
Async XLA Ops:
  0.6 1.0 %copy-start = (bf16[16,2,32,256]{3,2,1,0:T(8,128)(2,1)S(1)}, bf16[16,2,32,256]{3,2,1,0:T(8,128)(2,1)}, u32[]{:S(2)}) copy-start(bf16[16,2,32,256]{3,2,1,0:T(8,128)(2,1)} %vol_hbm.1) | copy-start | bytes 1572868
  2.1 5.2 %collective-permute-start = (bf16[6,16,256]{2,1,0:T(8,128)(2,1)S(1)}, bf16[6,16,256]{2,1,0:T(8,128)(2,1)S(1)}, u32[]{:S(2)}, u32[]{:S(2)}) collective-permute-start(bf16[6,16,256]{2,1,0:T(8,128)(2,1)S(1)} %get-tuple-element.23.after_ref), channel_id=1, source_target_pairs={{0,1},{1,0},{2,3},{3,2},{4,5},{5,4},{6,7},{7,6},{8,9},{9,8},{10,11... | collective-permute-start | bytes 147464 | tf_op jit(solution)/shard_map/ppermute | solution.py:312
  5.4 5.4 %collective-permute-start.1 = (bf16[6,16,256]{2,1,0:T(8,128)(2,1)S(1)}, bf16[6,16,256]{2,1,0:T(8,128)(2,1)S(1)}, u32[]{:S(2)}, u32[]{:S(2)}) collective-permute-start(bf16[6,16,256]{2,1,0:T(8,128)(2,1)S(1)} %get-tuple-element.26), channel_id=1, source_target_pairs={{1,2},{2,1},{5,6},{6,5},{9,10},{10,9},{13,14},{14,13},{17,18},{18,... | collective-permute-start | bytes 147464 | tf_op jit(solution)/shard_map/ppermute | solution.py:313
  10.8 8.2 %copy-start.1 = (bf16[16,1,64,128]{3,2,1,0:T(8,128)(2,1)S(1)}, bf16[16,1,64,128]{3,2,1,0:T(8,128)(2,1)}, u32[]{:S(2)}) copy-start(bf16[16,1,64,128]{3,2,1,0:T(8,128)(2,1)} %cot_ref.1) | copy-start | bytes 786436
  10.8 12.9 %collective-permute-start.2 = (bf16[38,16,256]{2,1,0:T(8,128)(2,1)S(1)}, bf16[38,16,256]{2,1,0:T(8,128)(2,1)S(1)}, u32[]{:S(2)}, u32[]{:S(2)}) collective-permute-start(bf16[38,16,256]{2,1,0:T(8,128)(2,1)S(1)} %get-tuple-element.27.b_ref), channel_id=1, source_target_pairs={{4,8},{8,4},{12,16},{16,12},{20,24},{24,20},{28,32},{32,28},{36,40... | collective-permute-start | bytes 933896 | tf_op jit(solution)/shard_map/ppermute | solution.py:294
  11.6 11.8 %copy-start.2 = (bf16[16,16,3,3,3]{1,0,4,3,2:T(8,128)(2,1)S(1)}, bf16[16,16,3,3,3]{1,0,4,3,2:T(8,128)(2,1)}, u32[]{:S(2)}) copy-start(bf16[16,16,3,3,3]{1,0,4,3,2:T(8,128)(2,1)} %param.5) | copy-start | bytes 41476
  11.6 17.1 %collective-permute-start.3 = (bf16[38,16,256]{2,1,0:T(8,128)(2,1)S(1)}, bf16[38,16,256]{2,1,0:T(8,128)(2,1)S(1)}, u32[]{:S(2)}, u32[]{:S(2)}) collective-permute-start(bf16[38,16,256]{2,1,0:T(8,128)(2,1)S(1)} %get-tuple-element.28.c_ref), channel_id=1, source_target_pairs={{0,4},{4,0},{8,12},{12,8},{16,20},{20,16},{24,28},{28,24},{32,36},... | collective-permute-start | bytes 933896 | tf_op jit(solution)/shard_map/ppermute | solution.py:293
  19.9 10.9 %all-to-all-start = ((bf16[4,18,16,128]{3,2,1,0:T(8,128)(2,1)}), bf16[4,18,16,128]{3,2,1,0:T(8,128)(2,1)S(1)}, u32[]{:S(2)}, u32[]{:S(2)}) async-start(bf16[4,18,16,128]{3,2,1,0:T(8,128)(2,1)} %shard_map.68), calls=%async_computation | async-start | bytes 589824 | tf_op jit(solution)/shard_map/all_to_all | solution.py:314
  23.7 7.2 %copy-start.3 = (bf16[64,16,3,3,3]{0,1,4,3,2:T(8,128)(2,1)S(1)}, bf16[64,16,3,3,3]{0,1,4,3,2:T(8,128)(2,1)}, u32[]{:S(2)}) copy-start(bf16[64,16,3,3,3]{0,1,4,3,2:T(8,128)(2,1)} %param.6) | copy-start | bytes 165892
  31.6 8.5 %collective-permute-start.4 = (bf16[34,16,128]{2,1,0:T(8,128)(2,1)S(1)}, bf16[34,16,128]{2,1,0:T(8,128)(2,1)S(1)}, u32[]{:S(2)}, u32[]{:S(2)}) collective-permute-start(bf16[34,16,128]{2,1,0:T(8,128)(2,1)S(1)} %get-tuple-element.31.after_ref.own_msg), channel_id=1, source_target_pairs={{0,4},{4,0},{8,12},{12,8},{16,20},{20,16},{24,28},{28,24},{32,36},... | collective-permute-start | bytes 417800 | tf_op jit(solution)/shard_map/ppermute | solution.py:293
  33.7 6.5 %collective-permute-start.5 = (bf16[34,16,128]{2,1,0:T(8,128)(2,1)S(1)}, bf16[34,16,128]{2,1,0:T(8,128)(2,1)S(1)}, u32[]{:S(2)}, u32[]{:S(2)}) collective-permute-start(bf16[34,16,128]{2,1,0:T(8,128)(2,1)S(1)} %get-tuple-element.32), channel_id=1, source_target_pairs={{4,8},{8,4},{12,16},{16,12},{20,24},{24,20},{28,32},{32,28},{36,40... | collective-permute-start | bytes 417800 | tf_op jit(solution)/shard_map/ppermute | solution.py:294
  79.4 10.2 %all-to-all-start.3 = ((bf16[16,16,256]{2,1,0:T(8,128)(2,1)}), bf16[16,16,256]{2,1,0:T(8,128)(2,1)S(1)}, u32[]{:S(2)}, u32[]{:S(2)}) async-start(bf16[16,16,256]{2,1,0:T(8,128)(2,1)} %shard_map.76), calls=%async_computation.3 | async-start | bytes 262144 | tf_op jit(solution)/shard_map/all_to_all | solution.py:299
  83.0 2.2 %collective-permute-start.6 = (bf16[16,16,128]{2,1,0:T(8,128)(2,1)S(1)}, bf16[16,16,128]{2,1,0:T(8,128)(2,1)S(1)}, u32[]{:S(2)}, u32[]{:S(2)}) collective-permute-start(bf16[16,16,128]{2,1,0:T(8,128)(2,1)S(1)} %get-tuple-element.37), channel_id=1, source_target_pairs={{0,1},{1,0},{2,3},{3,2},{4,5},{5,4},{6,7},{7,6},{8,9},{9,8},{10,11... | collective-permute-start | bytes 196616 | tf_op jit(solution)/shard_map/ppermute | solution.py:345
  83.1 3.5 %collective-permute-start.7 = (bf16[16,16,128]{2,1,0:T(8,128)(2,1)S(1)}, bf16[16,16,128]{2,1,0:T(8,128)(2,1)S(1)}, u32[]{:S(2)}, u32[]{:S(2)}) collective-permute-start(bf16[16,16,128]{2,1,0:T(8,128)(2,1)S(1)} %get-tuple-element.38), channel_id=1, source_target_pairs={{0,2},{1,3},{2,0},{3,1},{4,6},{5,7},{6,4},{7,5},{8,10},{9,11},{10,... | collective-permute-start | bytes 196616 | tf_op jit(solution)/shard_map/ppermute | solution.py:345
  83.4 5.4 %collective-permute-start.8 = (bf16[16,16,128]{2,1,0:T(8,128)(2,1)S(1)}, bf16[16,16,128]{2,1,0:T(8,128)(2,1)S(1)}, u32[]{:S(2)}, u32[]{:S(2)}) collective-permute-start(bf16[16,16,128]{2,1,0:T(8,128)(2,1)S(1)} %get-tuple-element.39), channel_id=1, source_target_pairs={{0,3},{1,2},{2,1},{3,0},{4,7},{5,6},{6,5},{7,4},{8,11},{9,10},{10,... | collective-permute-start | bytes 196616 | tf_op jit(solution)/shard_map/ppermute | solution.py:345
